TPU v7x, 16 devices: a whole 2x2x2 slice. The times are simulated.
16 devices in a mesh: data: 16 (over z, y, x, core).
Axes of the slice: x: 2, y: 2, z: 2, core: 2. Of those that a mesh axis runs over, the one named last changes fastest.
Arguments:
- x_tokens: bfloat16 [65536, 1024], P('data')
- dh_out: bfloat16 [65536, 1024], P('data')
- w_up: bfloat16 [2, 1024, 2736], replicated
- w_down: bfloat16 [2, 2736, 1024], replicated
- proj_up: bfloat16 [2, 1024, 256], replicated
- proj_down: bfloat16 [2, 1024, 256], replicated
- mom_up: float32 [2, 256, 2736], P(None, None, 'data')
- var_up: float32 [2, 256, 2736], P(None, None, 'data')
- mom_down: float32 [2, 2736, 256], P(None, 'data')
- var_down: float32 [2, 2736, 256], P(None, 'data')
Outputs:
- output 1: bfloat16 [2, 1024, 2736], replicated
- output 2: bfloat16 [2, 2736, 1024], replicated
- output 3: float32 [2, 256, 2736], P(None, None, 'data')
- output 4: float32 [2, 256, 2736], P(None, None, 'data')
- output 5: float32 [2, 2736, 256], P(None, 'data')
- output 6: float32 [2, 2736, 256], P(None, 'data')
All inputs are finite; a program needn't handle non-finite values.
Results may differ from a plain program's by a relative error of at most 0.00726549.
Values are sent between devices in bfloat16 or wider.
A program may use at most 1 GiB of HBM per device.

v0:
```python
import functools

import jax
import jax.numpy as jnp
from jax import lax
from jax.experimental import pallas as pl
from jax.experimental.pallas import tpu as pltpu
from jax.sharding import PartitionSpec as P

BETA_ONE = 0.9
BETA_TWO = 0.999
EPSILON = 1e-8
STEP = 4
LEARN_RATE = 0.02
ALPHA_SCALE = 0.25

C0 = 0.7978845608028654
C1 = C0 * 0.044715
D = 1024
FF = 2736
RANK = 256
DEV = 16
SHARD = FF // DEV
PAD = 176
FFP = DEV * PAD
F32 = jnp.float32
BF16 = jnp.bfloat16


def spans_of(width):
    return [(s, min(width, FF - s)) for s in range(0, FF, width)]


def dot_nn(a, b):
    return lax.dot_general(a, b, (((1,), (0,)), ((), ())), preferred_element_type=F32)


def dot_nt(a, b):
    return lax.dot_general(a, b, (((1,), (1,)), ((), ())), preferred_element_type=F32)


def gelu_val(z):
    z2 = z * z
    t = jnp.tanh(z * (C0 + C1 * z2))
    return z * (0.5 * t + 0.5)


def gelu_both(z):
    z2 = z * z
    t = jnp.tanh(z * (C0 + C1 * z2))
    c = 0.5 * t + 0.5
    a = z * c
    slope = c + (a - a * c) * (2.0 * C0 + 6.0 * C1 * z2)
    return a, slope


ANY = pl.BlockSpec(memory_space=pl.ANY)
ONCE = pl.Buffered(1)


def kernel_a(tile, tiles, x_ref, dh_ref, p_ref, q_ref, w1_hbm, w2_hbm,
             z0_hbm, g1_ref, u0_ref, r_hbm,
             w1a, w2a, w1b, w2b, z0, a0, h1, dz1, zs, das, ac, u1, v1, r1, r2, r3, rt, blk, sem, zsem):
    i = pl.program_id(0)
    width, slab = 512, 16
    spans = spans_of(width)
    loads = [
        pltpu.make_async_copy(w1_hbm.at[0], w1a, sem.at[0]),
        pltpu.make_async_copy(w2_hbm.at[0], w2a, sem.at[1]),
        pltpu.make_async_copy(w1_hbm.at[1], w1b, sem.at[2]),
        pltpu.make_async_copy(w2_hbm.at[1], w2b, sem.at[3]),
    ]

    def z_out(idx):
        return pltpu.make_async_copy(z0, z0_hbm.at[pl.ds(pl.multiple_of(idx * tile, tile), tile)], zsem)

    @pl.when(i == 0)
    def _():
        for cp in loads:
            cp.start()
        r1[...] = jnp.zeros_like(r1)
        r2[...] = jnp.zeros_like(r2)
        r3[...] = jnp.zeros_like(r3)

    x = x_ref[...]
    u0_ref[...] = dot_nn(x, p_ref[0]).T.astype(BF16)
    v1[...] = dot_nn(dh_ref[...], q_ref[1]).T.astype(BF16)

    @pl.when(i == 0)
    def _():
        loads[0].wait()

    @pl.when(i > 0)
    def _():
        z_out(i - 1).wait()

    def act0(span):
        s, w = span
        for r in range(0, tile, slab):
            a0[r:r + slab, s:s + w] = gelu_val(z0[r:r + slab, s:s + w]).astype(BF16)

    prev = None
    for span in spans:
        s, w = span
        z0[:, s:s + w] = dot_nt(x, w1a[s:s + w, :])
        if prev is not None:
            act0(prev)
        prev = span
    act0(prev)
    z_out(i).start()

    @pl.when(i == 0)
    def _():
        for cp in loads[1:]:
            cp.wait()

    for n in range(0, D, width):
        h1[:, n:n + width] = (x_ref[:, n:n + width].astype(F32) + dot_nn(a0[...], w2a[:, n:n + width])).astype(BF16)

    u1[...] = dot_nn(h1[...], p_ref[1]).T.astype(BF16)

    def act1(span, k):
        s, w = span
        for r in range(0, tile, slab):
            a, g = gelu_both(zs[k, r:r + slab, :w])
            ac[k, r:r + slab, :w] = a.astype(BF16)
            dz1[r:r + slab, s:s + w] = (g * das[k, r:r + slab, :w]).astype(BF16)

    def acc1(span, k):
        s, w = span
        r2[:, s:s + w] += dot_nn(v1[...], ac[k, :, :w])
        r1[:, s:s + w] += dot_nn(u1[...], dz1[:, s:s + w])

    h = h1[...]
    dh = dh_ref[...]
    spans = spans_of(256)
    n = len(spans)
    for j in range(n + 2):
        if j < n:
            s, w = spans[j]
            zs[j % 2, :, :w] = dot_nt(h, w1b[s:s + w, :])
            das[j % 2, :, :w] = dot_nt(dh, w2b[s:s + w, :])
        if 1 <= j <= n:
            act1(spans[j - 1], (j - 1) % 2)
        if j >= 2:
            acc1(spans[j - 2], (j - 2) % 2)

    for n in range(0, D, width):
        g1_ref[:, n:n + width] = (dh_ref[:, n:n + width].astype(F32) + dot_nn(dz1[...], w1b[:, n:n + width])).astype(BF16)
    v0 = dot_nn(g1_ref[...], q_ref[0]).T.astype(BF16)
    for s, w in spans:
        r3[:, s:s + w] += dot_nn(v0, a0[:, s:s + w])

    @pl.when(i == tiles - 1)
    def _():
        z_out(i).wait()
        for k, acc in enumerate((r1, r2, r3)):
            for s in range(0, FFP, 256):
                rt[s:s + 256, :] = acc[:, s:s + 256].T
            if k > 0:
                pltpu.make_async_copy(blk, r_hbm.at[:, (k - 1) * PAD:k * PAD, :], sem.at[k - 1]).wait()
            for d in range(DEV):
                blk[(d % 2) * 8 + d // 2] = rt[SHARD * d:SHARD * d + PAD, :]
            pltpu.make_async_copy(blk, r_hbm.at[:, k * PAD:(k + 1) * PAD, :], sem.at[k]).start()
        pltpu.make_async_copy(blk, r_hbm.at[:, 2 * PAD:, :], sem.at[2]).wait()


def call_a(x, dh, p, q, w1, w2):
    rows, tile = x.shape[0], 512
    tiles = rows // tile
    whole = pl.BlockSpec((2, D, RANK), lambda i: (0, 0, 0), pipeline_mode=ONCE)
    rowspec = pl.BlockSpec((tile, D), lambda i: (i, 0))
    colspec = pl.BlockSpec((RANK, tile), lambda i: (0, i))
    return pl.pallas_call(
        functools.partial(kernel_a, tile, tiles),
        grid=(tiles,),
        in_specs=[rowspec, rowspec, whole, whole, ANY, ANY],
        out_specs=[ANY, rowspec, colspec, ANY],
        out_shape=[
            jax.ShapeDtypeStruct((rows, FF), F32),
            jax.ShapeDtypeStruct((rows, D), BF16),
            jax.ShapeDtypeStruct((RANK, rows), BF16),
            jax.ShapeDtypeStruct((DEV, 3 * PAD, RANK), F32),
        ],
        scratch_shapes=[
            pltpu.VMEM((FF, D), BF16), pltpu.VMEM((FF, D), BF16),
            pltpu.VMEM((FF, D), BF16), pltpu.VMEM((FF, D), BF16),
            pltpu.VMEM((tile, FF), F32), pltpu.VMEM((tile, FF), BF16),
            pltpu.VMEM((tile, D), BF16), pltpu.VMEM((tile, FF), BF16),
            pltpu.VMEM((2, tile, 256), F32), pltpu.VMEM((2, tile, 256), F32), pltpu.VMEM((2, tile, 256), BF16),
            pltpu.VMEM((RANK, tile), BF16), pltpu.VMEM((RANK, tile), BF16),
            pltpu.VMEM((RANK, FFP), F32), pltpu.VMEM((RANK, FFP), F32), pltpu.VMEM((RANK, FFP), F32),
            pltpu.VMEM((FFP, RANK), F32), pltpu.VMEM((DEV, PAD, RANK), F32),
            pltpu.SemaphoreType.DMA((4,)), pltpu.SemaphoreType.DMA,
        ],
        compiler_params=pltpu.CompilerParams(
            dimension_semantics=("arbitrary",), vmem_limit_bytes=67000000),
        cost_estimate=pl.CostEstimate(flops=140 * 10**9, bytes_accessed=110 * 10**6, transcendentals=0),
        name="pass_a",
    )(x, dh, p, q, w1, w2)


def adam_shard(moment, variance, grad_red):
    new_mom = BETA_ONE * moment + (1.0 - BETA_ONE) * grad_red
    new_var = BETA_TWO * variance + (1.0 - BETA_TWO) * grad_red * grad_red
    bias_one = 1.0 - BETA_ONE ** STEP
    bias_two = 1.0 - BETA_TWO ** STEP
    direction = (new_mom / bias_one) / (jnp.sqrt(new_var / bias_two) + EPSILON)
    return new_mom, new_var, direction


AXES = ((2, 1, 0), (1, 0, 2), (0, 2, 1))
RS_Y = ((0, 56), (56, 56), (112, 64))
AG_Y = ((0, 48), (48, 64), (112, 64))
KIND_X = (1, 3, 2)
MESH = pl.DeviceIdType.MESH


def view(fixed, rows):
    return tuple(fixed.get(a, slice(None)) for a in range(3)) + (pl.ds(*rows), slice(None))


def kernel_d(tile, tiles, width, chunks,
             z0_ref, w2_ref, mu, vu, md, vd, g1_hbm, u0_hbm, rx_hbm,
             mu_o, vu_o, md_o, vd_o, n_hbm,
             g1, u0, das, dz, acc_s, racc, rt,
             own_x, x0, x1, x2, x3, own_y, y0, y1, y2, y3, gat, tmp, nb,
             lsem, rx_s, rx_r, ry_s, ry_r, ag_s, ag_r, nsem):
    j = pl.program_id(0)
    slab = 16
    me = lax.axis_index('data')
    bits = [lax.rem(me // (8 >> a), 2) for a in range(4)]
    peer = [me + (1 - 2 * bits[a]) * (8 >> a) for a in range(4)]
    core = bits[3]
    home = {a: bits[a] for a in range(3)}

    def remote(src, dst, s, r, axis):
        return pltpu.make_async_remote_copy(src_ref=src, dst_ref=dst, send_sem=s, recv_sem=r,
                                            device_id=(peer[axis],), device_id_type=MESH)

    def flow_x(h, p):
        return (lambda spot: own_x.at[spot], lambda spot: rx_hbm.at[(1 - core,) + spot], (x0, x1, x2, x3),
                (p * PAD + h * 88, 88), AXES[p], lambda st: (rx_s.at[h, p, st], rx_r.at[h, p, st]))

    def flow_y(p):
        return (lambda spot: own_y.at[(core,) + spot], lambda spot: own_y.at[(1 - core,) + spot], (y0, y1, y2, y3),
                RS_Y[p], AXES[p], lambda st: (ry_s.at[p, st], ry_r.at[p, st]))

    def rs_copy(flow, stage):
        own, away_src, bufs, rows, axes, sems = flow
        s, r = sems(stage)
        if stage == 0:
            spot = view({}, rows)
            return remote(away_src(spot), bufs[0].at[spot], s, r, 3)
        axis = axes[stage - 1]
        away = {a: bits[a] for a in axes[:stage - 1]}
        away[axis] = 1 - bits[axis]
        dst = bufs[stage].at[(slice(None),) * (3 - stage) + (pl.ds(*rows), slice(None))]
        return remote(own(view(away, rows)), dst, s, r, axis)

    def rs_step(flow, stage):
        own, _, bufs, rows, axes, _ = flow
        rs_copy(flow, stage).wait()
        ref = own(view({a: bits[a] for a in axes[:stage]}, rows))
        ref[...] = ref[...] + bufs[stage][(slice(None),) * (3 - stage) + (pl.ds(*rows), slice(None))]
        if stage < 3:
            rs_copy(flow, stage + 1).start()

    def ag_copy(kind, p, rows, slot):
        axes = AXES[p]
        if slot in (0, 1):
            at, axis = dict(home), (3 if slot == 0 else axes[0])
        elif slot in (2, 3):
            at, axis = {a: bits[a] for a in axes[slot - 1:]}, axes[slot - 1]
        else:
            st = slot - 3
            at, axis = {a: bits[a] for a in axes[st:]}, 3
            at[axes[st - 1]] = 1 - bits[axes[st - 1]]
        spot = gat.at[(kind, core) + view(at, rows)]
        return remote(spot, spot, ag_s.at[kind, p, slot], ag_r.at[kind, p, slot], axis)

    flows = [(KIND_X[p], p, (0, PAD)) for p in range(3)]
    flows_y = [(0, p, AG_Y[p]) for p in range(3)]

    def ag_begin(fl):
        ag_copy(*fl, 1).start()
        ag_copy(*fl, 0).start()

    def ag_step(fl, stage):
        ag_copy(*fl, stage).wait()
        if stage < 3:
            ag_copy(*fl, stage + 1).start()
        ag_copy(*fl, 3 + stage).start()

    def ag_end(fl):
        for slot in (0, 4, 5, 6):
            ag_copy(*fl, slot).wait()

    def adam(kind, grad):
        m_i, v_i, m_o, v_o = (mu, vu, mu_o, vu_o) if kind < 2 else (md, vd, md_o, vd_o)
        l = kind % 2
        new_mom, new_var, n = adam_shard(m_i[:, l, :], v_i[:, l, :], grad)
        m_o[:, l, :] = new_mom
        v_o[:, l, :] = new_var
        full = jnp.concatenate([n, jnp.zeros((PAD - SHARD, RANK), F32)], axis=0)
        gat[(kind, core, bits[0], bits[1], bits[2])] = full.astype(BF16)

    def n_copy(kind, slot):
        return pltpu.make_async_copy(nb.at[slot], n_hbm.at[kind], nsem.at[slot])

    def gather_rows(kind, slot):
        for d in range(DEV):
            block = gat[kind, d % 2, d // 8, d // 4 % 2, d // 2 % 2]
            tmp[SHARD * d:SHARD * (d + 1), :] = block.astype(F32)[:SHARD]
        nb[slot] = tmp[...].astype(BF16)
        n_copy(kind, slot).start()

    def local(k):
        src, dst = ((g1_hbm, g1), (u0_hbm, u0), (rx_hbm.at[core], own_x))[k]
        return pltpu.make_async_copy(src, dst, lsem.at[k])

    def begin():
        barrier = pltpu.get_barrier_semaphore()
        for a in range(4):
            pl.semaphore_signal(barrier, inc=1, device_id=(peer[a],), device_id_type=MESH)
        for k in range(3):
            local(k).start()
        pl.semaphore_wait(barrier, 4)
        for h in range(2):
            for p in range(3):
                rs_copy(flow_x(h, p), 0).start()
        local(0).wait()
        local(1).wait()

    def all_x(h, stage):
        for p in range(3):
            rs_step(flow_x(h, p), stage)

    def first_x():
        local(2).wait()
        all_x(0, 0)

    def finish_x():
        all_x(1, 3)
        for p in range(3):
            adam(KIND_X[p], own_x[bits[0], bits[1], bits[2], p * PAD:p * PAD + SHARD, :])
            ag_begin(flows[p])

    events = {0: begin, 1: first_x, 2: lambda: all_x(1, 0), 4: lambda: all_x(0, 1), 6: lambda: all_x(1, 1),
              7: lambda: all_x(0, 2), 8: lambda: all_x(1, 2), 9: lambda: all_x(0, 3), 10: finish_x}
    for at, event in events.items():
        pl.when(j == at)(event)

    now = lax.rem(j, 2)

    def turn(step):
        rt[pl.ds(pl.multiple_of(step * width, width), width), :] = racc[lax.rem(step, 2)].T

    def act(t):
        k = t % 2
        for r in range(0, tile, slab):
            slope = gelu_both(z0_ref[t * tile + r:t * tile + r + slab, :])[1]
            dz[k, r:r + slab, :] = (slope * das[k, r:r + slab, :]).astype(BF16)

    def acc(t):
        part = dot_nn(u0[:, t * tile:(t + 1) * tile], dz[t % 2])
        if t == tiles - 1:
            racc[now] = acc_s[...] + part
        else:
            acc_s[...] = part if t == 0 else acc_s[...] + part

    turn(lax.rem(j + chunks - 1, chunks))
    for t in range(tiles + 2):
        if t < tiles:
            das[t % 2] = dot_nt(g1[t * tile:(t + 1) * tile, :], w2_ref[...])
        if 1 <= t <= tiles:
            act(t - 1)
        if t >= 2:
            acc(t - 2)

    @pl.when(j == chunks - 1)
    def _():
        turn(j)
        for d in range(DEV):
            own_y[d % 2, d // 8, d // 4 % 2, d // 2 % 2] = rt[SHARD * d:SHARD * d + PAD, :]
        for p in range(3):
            rs_copy(flow_y(p), 0).start()
        for fl in flows:
            ag_step(fl, 1)
        for p in range(3):
            rs_step(flow_y(p), 0)
        for fl in flows:
            ag_step(fl, 2)
        for stage in (1, 2, 3):
            for p in range(3):
                rs_step(flow_y(p), stage)
        adam(0, own_y[core, bits[0], bits[1], bits[2], 0:SHARD, :])
        for fl in flows_y:
            ag_begin(fl)
        for fl in flows:
            ag_step(fl, 3)
        for fl in flows_y:
            ag_step(fl, 1)
        for p, fl in enumerate(flows):
            ag_end(fl)
            if p == 2:
                n_copy(KIND_X[0], 0).wait()
            gather_rows(KIND_X[p], p % 2)
            for other in flows_y if p < 2 else ():
                ag_step(other, 2 + p)
        for fl in flows_y:
            ag_end(fl)
        n_copy(KIND_X[1], 1).wait()
        gather_rows(0, 1)
        n_copy(KIND_X[2], 0).wait()
        n_copy(0, 1).wait()


def call_d(z0, g1, u0, w2, rx, mu, vu, md, vd):
    rows, tile, width = z0.shape[0], 512, 256
    chunks = FFP // width
    mom = jax.ShapeDtypeStruct((SHARD, 2, RANK), F32)
    momspec = pl.BlockSpec((SHARD, 2, RANK), lambda j: (0, 0, 0), pipeline_mode=ONCE)
    x, y = (2, 2, 2, 3 * PAD, RANK), (2, 2, 2, PAD, RANK)
    dma = pltpu.SemaphoreType.DMA
    return pl.pallas_call(
        functools.partial(kernel_d, tile, rows // tile, width, chunks),
        grid=(chunks,),
        in_specs=[
            pl.BlockSpec((rows, width), lambda j: (0, j)),
            pl.BlockSpec((None, width, D), lambda j: (0, j, 0)),
            momspec, momspec, momspec, momspec, ANY, ANY, ANY,
        ],
        out_specs=[momspec] * 4 + [ANY],
        out_shape=[mom] * 4 + [jax.ShapeDtypeStruct((4, FF, RANK), BF16)],
        scratch_shapes=[
            pltpu.VMEM((rows, D), BF16), pltpu.VMEM((RANK, rows), BF16),
            pltpu.VMEM((2, tile, width), F32), pltpu.VMEM((2, tile, width), BF16),
            pltpu.VMEM((RANK, width), F32), pltpu.VMEM((2, RANK, width), F32), pltpu.VMEM((FFP, RANK), F32),
            pltpu.VMEM(x, F32), pltpu.VMEM(x, F32), pltpu.VMEM(x[1:], F32), pltpu.VMEM(x[2:], F32), pltpu.VMEM(x[3:], F32),
            pltpu.VMEM((2,) + y, F32), pltpu.VMEM(y, F32), pltpu.VMEM(y[1:], F32), pltpu.VMEM(y[2:], F32), pltpu.VMEM(y[3:], F32),
            pltpu.VMEM((4, 2) + y, BF16), pltpu.VMEM((FF, RANK), F32), pltpu.VMEM((2, FF, RANK), BF16),
            dma((3,)), dma((2, 3, 4)), dma((2, 3, 4)), dma((3, 4)), dma((3, 4)), dma((4, 3, 7)), dma((4, 3, 7)), dma((2,)),
        ],
        compiler_params=pltpu.CompilerParams(
            dimension_semantics=("arbitrary",), collective_id=0, has_side_effects=True, vmem_limit_bytes=67000000),
        cost_estimate=pl.CostEstimate(flops=30 * 10**9, bytes_accessed=70 * 10**6, transcendentals=0),
        name="pass_d",
    )(z0, w2, mu, vu, md, vd, g1, u0, rx)


def kernel_w(w_ref, n_ref, p_ref, o_ref):
    n = n_ref[...]
    for s in range(0, D, 256):
        delta = dot_nt(n, p_ref[s:s + 256, :])
        o_ref[:, s:s + 256] = (w_ref[:, s:s + 256].astype(F32) - (LEARN_RATE * ALPHA_SCALE) * delta).astype(BF16)


def call_w(w, n, p, first):
    width = 912
    return pl.pallas_call(
        kernel_w,
        grid=(2, FF // width),
        in_specs=[
            pl.BlockSpec((None, width, D), lambda l, j: (l, j, 0)),
            pl.BlockSpec((None, width, RANK), lambda l, j: (first + l, j, 0)),
            pl.BlockSpec((None, D, RANK), lambda l, j: (l, 0, 0)),
        ],
        out_specs=pl.BlockSpec((None, width, D), lambda l, j: (l, j, 0)),
        out_shape=jax.ShapeDtypeStruct((2, FF, D), BF16),
        compiler_params=pltpu.CompilerParams(dimension_semantics=("arbitrary", "arbitrary")),
        cost_estimate=pl.CostEstimate(flops=3 * 10**9, bytes_accessed=23 * 10**6, transcendentals=0),
        name="pass_w",
    )(w, n, p)


def solution(mesh):
    def local_step(x_loc, dh_loc, w_up, w_down, proj_up, proj_down, mom_up, var_up, mom_down, var_down):
        w_up_t = jnp.swapaxes(w_up, 1, 2)
        z0, g1, u0, rx = call_a(x_loc, dh_loc, proj_up, proj_down, w_up_t, w_down)
        rx = rx.reshape(2, 2, 2, 2, 3 * PAD, RANK)
        up, down = (2, 0, 1), (1, 0, 2)
        mu, vu, md, vd, dirs = call_d(
            z0, g1, u0, w_down, rx, jnp.transpose(mom_up, up), jnp.transpose(var_up, up),
            jnp.transpose(mom_down, down), jnp.transpose(var_down, down))
        new_mom_up, new_var_up = jnp.transpose(mu, (1, 2, 0)), jnp.transpose(vu, (1, 2, 0))
        new_mom_down, new_var_down = jnp.transpose(md, (1, 0, 2)), jnp.transpose(vd, (1, 0, 2))
        new_w_up = jnp.swapaxes(call_w(w_up_t, dirs, proj_up, 0), 1, 2)
        new_w_down = call_w(w_down, dirs, proj_down, 2)
        return new_w_up, new_w_down, new_mom_up, new_var_up, new_mom_down, new_var_down

    tok_spec = P('data', None)
    up_spec = P(None, None, 'data')
    down_spec = P(None, 'data', None)
    return jax.shard_map(
        local_step,
        mesh=mesh,
        in_specs=(tok_spec, tok_spec, P(), P(), P(), P(), up_spec, up_spec, down_spec, down_spec),
        out_specs=(P(), P(), up_spec, up_spec, down_spec, down_spec),
        check_vma=False,
    )
```

profile of v0, /device:TPU:0, one launch (start us, length us, event | category | flops | bytes accessed | tf_op | source)
XLA Modules:
  0.0 308.7 jit_solution(11030579115960305958)
XLA Ops:
  0.6 181.5 %pass_a.1 = (f32[4096,2736]{1,0:T(8,128)}, bf16[4096,1024]{1,0:T(8,128)(2,1)}, bf16[256,4096]{1,0:T(8,128)(2,1)}, f32[16,528,256]{2,1,0:T(8,128)}) custom-call(bf16[4096,1024]{1,0:T(8,128)(2,1)} %x_ref.1, bf16[4096,1024]{1,0:T(8,128)(2,1)} %dh_ref.1, bf16[2,1024,256]{2,1,0:T(8,128)(2,1)} %p_ref.4, bf16[2,1024,256]{2,1,0:T(8,128)(2,1)} %p_ref.5, ...), custom_call_target="tpu_custom_call" | custom-call | flops 140000002048 | bytes 110000000 | tf_op jit(solution)/shard_map/pass_a/pallas_call | solution.py:174
  182.2 99.7 %pass_d.1 = (f32[171,2,256]{2,1,0:T(2,128)}, f32[171,2,256]{2,1,0:T(2,128)}, f32[171,2,256]{2,1,0:T(2,128)}, f32[171,2,256]{2,1,0:T(2,128)}, bf16[4,2736,256]{2,1,0:T(8,128)(2,1)}) custom-call(f32[4096,2736]{1,0:T(8,128)} %get-tuple-element.15.z0_ref, bf16[2,2736,1024]{2,1,0:T(8,128)(2,1)} %w_ref.1, f32[171,2,256]{2,1,0:T(2,128)} %bitcast.18, ...), custom_call_target="tpu_custom_call" | custom-call | flops 30000001024 | bytes 70000000 | tf_op jit(solution)/shard_map/pass_d/pallas_call | solution.py:426
  281.9 11.9 %pass_w.3 = bf16[2,2736,1024]{2,1,0:T(8,128)(2,1)} custom-call(bf16[2,2736,1024]{2,1,0:T(8,128)(2,1)} %w_ref.1, bf16[4,2736,256]{2,1,0:T(8,128)(2,1)} %get-tuple-element.19.n_ref, bf16[2,1024,256]{2,1,0:T(8,128)(2,1)} %p_ref.5), custom_call_target="tpu_custom_call" | custom-call | flops 3000000000 | bytes 23000000 | tf_op jit(solution)/shard_map/pass_w/pallas_call | solution.py:461
  293.8 0.0 copy-start.3
  293.8 0.0 copy-start.2
  293.8 0.0 copy-start.1
  293.8 0.0 copy-start
  293.8 12.0 %pass_w.2 = bf16[2,2736,1024]{2,1,0:T(8,128)(2,1)} custom-call(bf16[2,2736,1024]{2,1,0:T(8,128)(2,1)} %bitcast.12, bf16[4,2736,256]{2,1,0:T(8,128)(2,1)} %get-tuple-element.19.n_ref, bf16[2,1024,256]{2,1,0:T(8,128)(2,1)} %p_ref.4), custom_call_target="tpu_custom_call" | custom-call | flops 3000000000 | bytes 23000000 | tf_op jit(solution)/shard_map/pass_w/pallas_call | solution.py:461
  305.8 0.0 copy-done.3
  305.8 0.7 copy.20
  306.5 0.0 copy-done.2
  306.5 0.7 copy.21
  307.2 0.0 copy-done.1
  307.2 0.7 copy.22
  308.0 0.0 copy-done
  308.0 0.7 copy.23
Async XLA Ops:
  293.8 12.0 %copy-start.3 = (f32[171,2,256]{2,1,0:T(2,128)S(1)}, f32[171,2,256]{2,1,0:T(2,128)}, u32[]{:S(2)}) copy-start(f32[171,2,256]{2,1,0:T(2,128)} %get-tuple-element.20) | copy-start | bytes 1050628
  293.8 12.7 %copy-start.2 = (f32[171,2,256]{2,1,0:T(2,128)S(1)}, f32[171,2,256]{2,1,0:T(2,128)}, u32[]{:S(2)}) copy-start(f32[171,2,256]{2,1,0:T(2,128)} %get-tuple-element.21) | copy-start | bytes 1050628
  293.8 13.5 %copy-start.1 = (f32[171,2,256]{2,1,0:T(2,128)S(1)}, f32[171,2,256]{2,1,0:T(2,128)}, u32[]{:S(2)}) copy-start(f32[171,2,256]{2,1,0:T(2,128)} %get-tuple-element.22) | copy-start | bytes 1050628
  293.8 14.2 %copy-start = (f32[171,2,256]{2,1,0:T(2,128)S(1)}, f32[171,2,256]{2,1,0:T(2,128)}, u32[]{:S(2)}) copy-start(f32[171,2,256]{2,1,0:T(2,128)} %get-tuple-element.23) | copy-start | bytes 1050628
where the time goes:
time: 309 us
  Pallas kernels  305 us (99%)
    pallas_call x1, Pallas kernels, call_a(): pl.pallas_call(functools.partial(kernel_a, tile, tiles), grid=(tiles,), i...  182 us
    pallas_call x1, Pallas kernels, call_d(): pl.pallas_call(functools.partial(kernel_d, tile, rows // tile, width, chu...  99.7 us
    pallas_call x2, Pallas kernels, call_w(): pl.pallas_call(kernel_w, grid=(2, FF // width), in_specs=[pl.BlockSpec((N...  23.8 us

commit v1 on v0

v1 whole, which is shorter than its diff:
```python
import functools

import jax
import jax.numpy as jnp
from jax import lax
from jax.experimental import pallas as pl
from jax.experimental.pallas import tpu as pltpu
from jax.sharding import PartitionSpec as P

BETA_ONE = 0.9
BETA_TWO = 0.999
EPSILON = 1e-8
STEP = 4
LEARN_RATE = 0.02
ALPHA_SCALE = 0.25

C0 = 0.7978845608028654
C1 = C0 * 0.044715
D = 1024
FF = 2736
RANK = 256
DEV = 16
SHARD = FF // DEV
PAD = 176
FFP = DEV * PAD
F32 = jnp.float32
BF16 = jnp.bfloat16


def spans_of(width):
    return [(s, min(width, FF - s)) for s in range(0, FF, width)]


def dot_nn(a, b):
    return lax.dot_general(a, b, (((1,), (0,)), ((), ())), preferred_element_type=F32)


def dot_nt(a, b):
    return lax.dot_general(a, b, (((1,), (1,)), ((), ())), preferred_element_type=F32)


def gelu_val(z):
    z2 = z * z
    t = jnp.tanh(z * (C0 + C1 * z2))
    return z * (0.5 * t + 0.5)


def gelu_both(z):
    z2 = z * z
    t = jnp.tanh(z * (C0 + C1 * z2))
    c = 0.5 * t + 0.5
    a = z * c
    slope = c + (a - a * c) * (2.0 * C0 + 6.0 * C1 * z2)
    return a, slope


ANY = pl.BlockSpec(memory_space=pl.ANY)
ONCE = pl.Buffered(1)


def kernel_a(tile, tiles, x_ref, dh_ref, p_ref, q_ref, w1_hbm, w2_hbm,
             z0_hbm, a0_hbm, dz1, u0_ref, r_hbm,
             w1a, w2a, w1b, w2b, z0, a0, h1, zs, das, ac, u1, v1, r1, r2, blk, sem, zsem):
    i = pl.program_id(0)
    width, slab = 512, 16
    spans = spans_of(width)
    loads = [
        pltpu.make_async_copy(w1_hbm.at[0], w1a, sem.at[0]),
        pltpu.make_async_copy(w2_hbm.at[0], w2a, sem.at[1]),
        pltpu.make_async_copy(w1_hbm.at[1], w1b, sem.at[2]),
        pltpu.make_async_copy(w2_hbm.at[1], w2b, sem.at[3]),
    ]

    def out(idx, k):
        src, dst = ((z0, z0_hbm), (a0, a0_hbm))[k]
        return pltpu.make_async_copy(src, dst.at[pl.ds(pl.multiple_of(idx * tile, tile), tile)], zsem.at[k])

    @pl.when(i == 0)
    def _():
        for cp in loads:
            cp.start()
        r1[...] = jnp.zeros_like(r1)
        r2[...] = jnp.zeros_like(r2)
        for cp in loads:
            cp.wait()

    @pl.when(i > 0)
    def _():
        out(i - 1, 0).wait()
        out(i - 1, 1).wait()

    x = x_ref[...]
    dh = dh_ref[...]

    def act0(span):
        s, w = span
        for r in range(0, tile, slab):
            a0[r:r + slab, s:s + w] = gelu_val(z0[r:r + slab, s:s + w]).astype(BF16)

    prev = None
    for span in spans:
        s, w = span
        z0[:, s:s + w] = dot_nt(x, w1a[s:s + w, :])
        if prev is not None:
            act0(prev)
        prev = span
    u0_ref[...] = dot_nt(p_ref[0], x).astype(BF16)
    v1[...] = dot_nt(q_ref[1], dh).astype(BF16)
    act0(prev)

    for n in range(0, D, width):
        h1[:, n:n + width] = (x_ref[:, n:n + width].astype(F32) + dot_nn(a0[...], w2a[:, n:n + width])).astype(BF16)
    out(i, 0).start()
    out(i, 1).start()

    def act1(span, k):
        s, w = span
        for r in range(0, tile, slab):
            a, g = gelu_both(zs[k, r:r + slab, :w])
            ac[k, r:r + slab, :w] = a.astype(BF16)
            dz1[r:r + slab, s:s + w] = (g * das[k, r:r + slab, :w]).astype(BF16)

    def acc1(span, k):
        s, w = span
        r2[:, s:s + w] += dot_nn(v1[...], ac[k, :, :w])
        r1[:, s:s + w] += dot_nn(u1[...], dz1[:, s:s + w])

    h = h1[...]
    n = len(spans)
    for j in range(n + 2):
        if j < n:
            s, w = spans[j]
            das[j % 2, :, :w] = dot_nt(dh, w2b[s:s + w, :])
            zs[j % 2, :, :w] = dot_nt(h, w1b[s:s + w, :])
        if j == 0:
            u1[...] = dot_nt(p_ref[1], h).astype(BF16)
        if 1 <= j <= n:
            act1(spans[j - 1], (j - 1) % 2)
        if j >= 2:
            acc1(spans[j - 2], (j - 2) % 2)

    @pl.when(i == tiles - 1)
    def _():
        out(i, 0).wait()
        out(i, 1).wait()
        for k, acc in enumerate((r1, r2)):
            for t in range(FFP // 256):
                z0[t % 2 * 256:t % 2 * 256 + 256, t // 2 * 256:t // 2 * 256 + 256] = acc[:, t * 256:t * 256 + 256].T
            if k == 1:
                pltpu.make_async_copy(blk, r_hbm.at[0], sem.at[0]).wait()
            for d in range(DEV):
                row, end = SHARD * d, SHARD * d + PAD
                while row < end:
                    t, lo = row // 256, row % 256
                    take = min(end - row, 256 - lo)
                    to = row - SHARD * d
                    blk[(d % 2) * 8 + d // 2, to:to + take, :] = z0[t % 2 * 256 + lo:t % 2 * 256 + lo + take, t // 2 * 256:t // 2 * 256 + 256]
                    row += take
            pltpu.make_async_copy(blk, r_hbm.at[k], sem.at[k]).start()
        pltpu.make_async_copy(blk, r_hbm.at[1], sem.at[1]).wait()


def leave(acc, rt):
    for s in range(0, FFP, 256):
        rt[s:s + 256, :] = acc[:, s:s + 256].T


def call_a(x, dh, p, q, w1, w2):
    rows, tile = x.shape[0], 512
    tiles = rows // tile
    whole = pl.BlockSpec((2, RANK, D), lambda i: (0, 0, 0), pipeline_mode=ONCE)
    rowspec = pl.BlockSpec((tile, D), lambda i: (i, 0))
    return pl.pallas_call(
        functools.partial(kernel_a, tile, tiles),
        grid=(tiles,),
        in_specs=[rowspec, rowspec, whole, whole, ANY, ANY],
        out_specs=[ANY, ANY, pl.BlockSpec((tile, FF), lambda i: (i, 0)), pl.BlockSpec((RANK, tile), lambda i: (0, i)), ANY],
        out_shape=[
            jax.ShapeDtypeStruct((rows, FF), F32),
            jax.ShapeDtypeStruct((rows, FF), BF16),
            jax.ShapeDtypeStruct((rows, FF), BF16),
            jax.ShapeDtypeStruct((RANK, rows), BF16),
            jax.ShapeDtypeStruct((2, DEV, PAD, RANK), F32),
        ],
        scratch_shapes=[
            pltpu.VMEM((FF, D), BF16), pltpu.VMEM((FF, D), BF16),
            pltpu.VMEM((FF, D), BF16), pltpu.VMEM((FF, D), BF16),
            pltpu.VMEM((tile, FF), F32), pltpu.VMEM((tile, FF), BF16), pltpu.VMEM((tile, D), BF16),
            pltpu.VMEM((2, tile, 512), F32), pltpu.VMEM((2, tile, 512), F32), pltpu.VMEM((2, tile, 512), BF16),
            pltpu.VMEM((RANK, tile), BF16), pltpu.VMEM((RANK, tile), BF16),
            pltpu.VMEM((RANK, FFP), F32), pltpu.VMEM((RANK, FFP), F32),
            pltpu.VMEM((DEV, PAD, RANK), F32),
            pltpu.SemaphoreType.DMA((4,)), pltpu.SemaphoreType.DMA((2,)),
        ],
        compiler_params=pltpu.CompilerParams(
            dimension_semantics=("arbitrary",), vmem_limit_bytes=67000000),
        cost_estimate=pl.CostEstimate(flops=110 * 10**9, bytes_accessed=140 * 10**6, transcendentals=0),
        name="pass_a",
    )(x, dh, p, q, w1, w2)


def adam_shard(moment, variance, grad_red):
    new_mom = BETA_ONE * moment + (1.0 - BETA_ONE) * grad_red
    new_var = BETA_TWO * variance + (1.0 - BETA_TWO) * grad_red * grad_red
    bias_one = 1.0 - BETA_ONE ** STEP
    bias_two = 1.0 - BETA_TWO ** STEP
    direction = (new_mom / bias_one) / (jnp.sqrt(new_var / bias_two) + EPSILON)
    return new_mom, new_var, direction


AXES = ((2, 1, 0), (1, 0, 2), (0, 2, 1))
RS_ROWS = ((0, 56), (56, 56), (112, 64))
AG_ROWS = ((0, 48), (48, 64), (112, 64))
MESH = pl.DeviceIdType.MESH
CUBE = (2, 2, 2, PAD, RANK)


def view(fixed, rows):
    return tuple(fixed.get(a, slice(None)) for a in range(3)) + (pl.ds(*rows), slice(None))


class Comm:
    def __init__(self):
        me = lax.axis_index('data')
        self.bits = [lax.rem(me // (8 >> a), 2) for a in range(4)]
        self.peer = [me + (1 - 2 * self.bits[a]) * (8 >> a) for a in range(4)]
        self.core = self.bits[3]

    def greet(self):
        barrier = pltpu.get_barrier_semaphore()
        for a in range(4):
            pl.semaphore_signal(barrier, inc=1, device_id=(self.peer[a],), device_id_type=MESH)

    def met(self):
        pl.semaphore_wait(pltpu.get_barrier_semaphore(), 4)

    def remote(self, src, dst, s, r, axis):
        return pltpu.make_async_remote_copy(src_ref=src, dst_ref=dst, send_sem=s, recv_sem=r,
                                            device_id=(self.peer[axis],), device_id_type=MESH)

    def rs_copy(self, flow, stage):
        own, other, bufs, sems, p = flow
        rows, axes = RS_ROWS[p], AXES[p]
        s, r = (sem.at[p, stage] for sem in sems)
        if stage == 0:
            spot = view({}, rows)
            return self.remote(other.at[spot], bufs[0].at[spot], s, r, 3)
        axis = axes[stage - 1]
        away = {a: self.bits[a] for a in axes[:stage - 1]}
        away[axis] = 1 - self.bits[axis]
        dst = bufs[stage].at[(slice(None),) * (3 - stage) + (pl.ds(*rows), slice(None))]
        return self.remote(own.at[view(away, rows)], dst, s, r, axis)

    def rs_step(self, flow, stage):
        own, _, bufs, _, p = flow
        rows, axes = RS_ROWS[p], AXES[p]
        self.rs_copy(flow, stage).wait()
        ref = own.at[view({a: self.bits[a] for a in axes[:stage]}, rows)]
        ref[...] = ref[...] + bufs[stage][(slice(None),) * (3 - stage) + (pl.ds(*rows), slice(None))]
        if stage < 3:
            self.rs_copy(flow, stage + 1).start()

    def ag_copy(self, gat, sems, kind, p, slot):
        rows, axes, bits = AG_ROWS[p], AXES[p], self.bits
        if slot == 0:
            at, axis = {a: bits[a] for a in range(3)}, 3
        elif slot <= 3:
            at, axis = {a: bits[a] for a in axes[slot - 1:]}, axes[slot - 1]
        else:
            at, axis = {a: bits[a] for a in axes[slot - 3:]}, 3
            at[axes[slot - 4]] = 1 - bits[axes[slot - 4]]
        spot = gat.at[(kind, self.core) + view(at, rows)]
        return self.remote(spot, spot, sems[0].at[kind, p, slot], sems[1].at[kind, p, slot], axis)

    def ag_begin(self, *flow):
        self.ag_copy(*flow, 1).start()
        self.ag_copy(*flow, 0).start()

    def ag_step(self, *flow, stage):
        self.ag_copy(*flow, stage).wait()
        if stage < 3:
            self.ag_copy(*flow, stage + 1).start()
        self.ag_copy(*flow, 3 + stage).start()

    def ag_end(self, *flow):
        for slot in (0, 4, 5, 6):
            self.ag_copy(*flow, slot).wait()


def stages():
    return [pltpu.VMEM(CUBE[k:], F32) if k else pltpu.VMEM(CUBE, F32) for k in range(4)]


def kernel_c(tile, tiles, dh_ref, dz_ref, a0_ref, w1_ref, q_ref, rx_hbm,
             g1_ref, sum_ref, ry_hbm,
             r3, rt, blk, own, xa0, xa1, xa2, xa3, xb0, xb1, xb2, xb3, lsem, as_, ar, bs, br):
    i = pl.program_id(0)
    c = Comm()
    bufs = ((xa0, xa1, xa2, xa3), (xb0, xb1, xb2, xb3))
    sems = ((as_, ar), (bs, br))
    flows = [(own.at[k], rx_hbm.at[k, 1 - c.core], bufs[k], sems[k], p) for k in range(2) for p in range(3)]

    def mine():
        return pltpu.make_async_copy(rx_hbm.at[:, c.core], own, lsem.at[0])

    @pl.when(i == 0)
    def _():
        c.greet()
        mine().start()
        r3[...] = jnp.zeros_like(r3)
        c.met()
        for flow in flows:
            c.rs_copy(flow, 0).start()

    @pl.when(i == 2)
    def _():
        mine().wait()

    for at, stage in ((2, 0), (5, 1), (7, 2)):
        @pl.when(i == at)
        def _():
            for flow in flows:
                c.rs_step(flow, stage)

    half = 512
    for n in range(0, D, half):
        g1_ref[:, n:n + half] = (dh_ref[:, n:n + half].astype(F32) + dot_nn(dz_ref[...], w1_ref[:, n:n + half])).astype(BF16)
    v0 = dot_nt(q_ref[...], g1_ref[...]).astype(BF16)
    for s, w in spans_of(512):
        r3[:, s:s + w] += dot_nn(v0, a0_ref[:, s:s + w])

    @pl.when(i == tiles - 1)
    def _():
        leave(r3, rt)
        for d in range(DEV):
            blk[(d % 2) * 8 + d // 2] = rt[SHARD * d:SHARD * d + PAD, :]
        out = pltpu.make_async_copy(blk, ry_hbm, lsem.at[0])
        out.start()
        for flow in flows:
            c.rs_step(flow, 3)
        for k in range(2):
            sum_ref[k] = own[k, c.bits[0], c.bits[1], c.bits[2]]
        out.wait()


def call_c(dh, dz, a0, w1, q, rx):
    rows, tile = dh.shape[0], 512
    tiles = rows // tile
    dma = pltpu.SemaphoreType.DMA
    return pl.pallas_call(
        functools.partial(kernel_c, tile, tiles),
        grid=(tiles,),
        in_specs=[
            pl.BlockSpec((tile, D), lambda i: (i, 0)),
            pl.BlockSpec((tile, FF), lambda i: (i, 0)),
            pl.BlockSpec((tile, FF), lambda i: (i, 0)),
            pl.BlockSpec((None, FF, D), lambda i: (1, 0, 0), pipeline_mode=ONCE),
            pl.BlockSpec((None, RANK, D), lambda i: (0, 0, 0), pipeline_mode=ONCE),
            ANY,
        ],
        out_specs=[
            pl.BlockSpec((tile, D), lambda i: (i, 0)),
            pl.BlockSpec((2, PAD, RANK), lambda i: (0, 0, 0), pipeline_mode=ONCE),
            ANY,
        ],
        out_shape=[
            jax.ShapeDtypeStruct((rows, D), BF16),
            jax.ShapeDtypeStruct((2, PAD, RANK), F32),
            jax.ShapeDtypeStruct((DEV, PAD, RANK), F32),
        ],
        scratch_shapes=[
            pltpu.VMEM((RANK, FFP), F32), pltpu.VMEM((FFP, RANK), F32), pltpu.VMEM((DEV, PAD, RANK), F32),
            pltpu.VMEM((2,) + CUBE, F32), *stages(), *stages(),
            dma((1,)), dma((3, 4)), dma((3, 4)), dma((3, 4)), dma((3, 4)),
        ],
        compiler_params=pltpu.CompilerParams(
            dimension_semantics=("arbitrary",), collective_id=1, has_side_effects=True, vmem_limit_bytes=60000000),
        cost_estimate=pl.CostEstimate(flops=31 * 10**9, bytes_accessed=70 * 10**6, transcendentals=0),
        name="pass_c",
    )(dh, dz, a0, w1, q, rx)


def kernel_d(tile, tiles, width, chunks,
             z0_ref, w2_ref, sum_ref, mu, vu, md, vd, g1_hbm, u0_hbm, rx_hbm,
             mu_o, vu_o, md_o, vd_o, n_hbm,
             g1, u0, das, dz, acc_s, racc, rt, own_x, own_y,
             x0, x1, x2, x3, y0, y1, y2, y3, gat, tmp, nb,
             lsem, rx_s, rx_r, ry_s, ry_r, ag_s, ag_r, nsem):
    j = pl.program_id(0)
    slab = 16
    c = Comm()
    bits, core = c.bits, c.core
    ag_sems = (ag_s, ag_r)
    flows_x = [(own_x, rx_hbm.at[1 - core], (x0, x1, x2, x3), (rx_s, rx_r), p) for p in range(3)]
    flows_y = [(own_y.at[core], own_y.at[1 - core], (y0, y1, y2, y3), (ry_s, ry_r), p) for p in range(3)]

    def rs(flows, stage):
        for flow in flows:
            c.rs_step(flow, stage)

    def ag(kinds, stage):
        for kind in kinds:
            for p in range(3):
                if stage == 0:
                    c.ag_begin(gat, ag_sems, kind, p)
                elif stage < 4:
                    c.ag_step(gat, ag_sems, kind, p, stage=stage)
                else:
                    c.ag_end(gat, ag_sems, kind, p)

    def adam(kind, grad):
        m_i, v_i, m_o, v_o = (mu, vu, mu_o, vu_o) if kind < 2 else (md, vd, md_o, vd_o)
        l = kind % 2
        new_mom, new_var, n = adam_shard(m_i[:, l, :], v_i[:, l, :], grad)
        m_o[:, l, :] = new_mom
        v_o[:, l, :] = new_var
        full = jnp.concatenate([n, jnp.zeros((PAD - SHARD, RANK), F32)], axis=0)
        gat[(kind, core, bits[0], bits[1], bits[2])] = full.astype(BF16)

    def n_copy(kind):
        return pltpu.make_async_copy(nb.at[kind % 2], n_hbm.at[kind], nsem.at[kind])

    def gather_rows(kind):
        for d in range(DEV):
            block = gat[kind, d % 2, d // 8, d // 4 % 2, d // 2 % 2]
            tmp[SHARD * d:SHARD * (d + 1), :] = block.astype(F32)[:SHARD]
        nb[kind % 2] = tmp[...].astype(BF16)
        n_copy(kind).start()

    def local(k):
        src, dst = ((g1_hbm, g1), (u0_hbm, u0), (rx_hbm.at[core], own_x))[k]
        return pltpu.make_async_copy(src, dst, lsem.at[k])

    def begin():
        c.greet()
        for k in range(3):
            local(k).start()
        adam(1, sum_ref[0, 0:SHARD, :])
        adam(3, sum_ref[1, 0:SHARD, :])
        c.met()
        ag((1, 3), 0)
        for flow in flows_x:
            c.rs_copy(flow, 0).start()
        for k in range(3):
            local(k).wait()

    def step_one():
        rs(flows_x, 0)
        ag((1, 3), 1)

    def finish_x():
        rs(flows_x, 3)
        adam(2, own_x[bits[0], bits[1], bits[2], 0:SHARD, :])
        ag((2,), 0)

    events = {0: begin, 1: step_one, 2: lambda: ag((1, 3), 2), 3: lambda: rs(flows_x, 1), 4: lambda: ag((1, 3), 3),
              5: lambda: rs(flows_x, 2), 7: finish_x, 8: lambda: ag((2,), 1), 9: lambda: ag((2,), 2), 10: lambda: ag((2,), 3)}
    for at, event in events.items():
        pl.when(j == at)(event)

    now = lax.rem(j, 2)

    def turn(step):
        rt[pl.ds(pl.multiple_of(step * width, width), width), :] = racc[lax.rem(step, 2)].T

    def act(t):
        k = t % 2
        for r in range(0, tile, slab):
            slope = gelu_both(z0_ref[t * tile + r:t * tile + r + slab, :])[1]
            dz[k, r:r + slab, :] = (slope * das[k, r:r + slab, :]).astype(BF16)

    def acc(t):
        part = dot_nn(u0[:, t * tile:(t + 1) * tile], dz[t % 2])
        if t == tiles - 1:
            racc[now] = acc_s[...] + part
        else:
            acc_s[...] = part if t == 0 else acc_s[...] + part

    turn(lax.rem(j + chunks - 1, chunks))
    for t in range(tiles + 2):
        if t < tiles:
            das[t % 2] = dot_nt(g1[t * tile:(t + 1) * tile, :], w2_ref[...])
        if 1 <= t <= tiles:
            act(t - 1)
        if t >= 2:
            acc(t - 2)

    @pl.when(j == chunks - 1)
    def _():
        turn(j)
        for d in range(DEV):
            own_y[d % 2, d // 8, d // 4 % 2, d // 2 % 2] = rt[SHARD * d:SHARD * d + PAD, :]
        for flow in flows_y:
            c.rs_copy(flow, 0).start()
        ag((1, 3), 4)
        gather_rows(1)
        rs(flows_y, 0)
        ag((2,), 4)
        gather_rows(2)
        rs(flows_y, 1)
        n_copy(1).wait()
        gather_rows(3)
        rs(flows_y, 2)
        rs(flows_y, 3)
        adam(0, own_y[core, bits[0], bits[1], bits[2], 0:SHARD, :])
        for stage in range(5):
            ag((0,), stage)
        n_copy(2).wait()
        gather_rows(0)
        n_copy(3).wait()
        n_copy(0).wait()


def call_d(z0, g1, u0, w2, sums, rx, mu, vu, md, vd):
    rows, tile, width = z0.shape[0], 512, 256
    chunks = FFP // width
    mom = jax.ShapeDtypeStruct((SHARD, 2, RANK), F32)
    momspec = pl.BlockSpec((SHARD, 2, RANK), lambda j: (0, 0, 0), pipeline_mode=ONCE)
    dma = pltpu.SemaphoreType.DMA
    return pl.pallas_call(
        functools.partial(kernel_d, tile, rows // tile, width, chunks),
        grid=(chunks,),
        in_specs=[
            pl.BlockSpec((rows, width), lambda j: (0, j)),
            pl.BlockSpec((None, width, D), lambda j: (0, j, 0)),
            pl.BlockSpec((2, PAD, RANK), lambda j: (0, 0, 0), pipeline_mode=ONCE),
            momspec, momspec, momspec, momspec, ANY, ANY, ANY,
        ],
        out_specs=[momspec] * 4 + [ANY],
        out_shape=[mom] * 4 + [jax.ShapeDtypeStruct((4, FF, RANK), BF16)],
        scratch_shapes=[
            pltpu.VMEM((rows, D), BF16), pltpu.VMEM((RANK, rows), BF16),
            pltpu.VMEM((2, tile, width), F32), pltpu.VMEM((2, tile, width), BF16),
            pltpu.VMEM((RANK, width), F32), pltpu.VMEM((2, RANK, width), F32), pltpu.VMEM((FFP, RANK), F32),
            pltpu.VMEM(CUBE, F32), pltpu.VMEM((2,) + CUBE, F32), *stages(), *stages(),
            pltpu.VMEM((4, 2) + CUBE, BF16), pltpu.VMEM((FF, RANK), F32), pltpu.VMEM((2, FF, RANK), BF16),
            dma((3,)), dma((3, 4)), dma((3, 4)), dma((3, 4)), dma((3, 4)), dma((4, 3, 7)), dma((4, 3, 7)), dma((4,)),
        ],
        compiler_params=pltpu.CompilerParams(
            dimension_semantics=("arbitrary",), collective_id=0, has_side_effects=True, vmem_limit_bytes=67000000),
        cost_estimate=pl.CostEstimate(flops=30 * 10**9, bytes_accessed=70 * 10**6, transcendentals=0),
        name="pass_d",
    )(z0, w2, sums, mu, vu, md, vd, g1, u0, rx)


def kernel_w(count, part, wu_hbm, wd_hbm, n_hbm, p_ref, q_ref, nu_hbm, nd_hbm, buf, n, isem, nsem, osem):
    per = FF // part

    def load(k):
        src, at = (wu_hbm, k) if k < 2 * per else (wd_hbm, k - 2 * per)
        return pltpu.make_async_copy(src.at[at], buf.at[k], isem.at[k])

    def names(kind):
        return pltpu.make_async_copy(n_hbm.at[pl.ds(kind * per, per)], n.at[pl.ds(kind * per, per)], nsem.at[kind])

    for k in range(count):
        if k % per == 0:
            names(k // per).start()
        load(k).start()
    for kind in range(4):
        proj, dst, base = (p_ref, nu_hbm, 0) if kind < 2 else (q_ref, nd_hbm, 2 * per)
        names(kind).wait()

        def body(t, carry):
            k = kind * per + t
            pltpu.make_async_copy(wu_hbm.at[0], buf.at[k], isem.at[k]).wait()
            for s in range(0, D, 256):
                delta = dot_nt(n[k], proj[kind % 2, s:s + 256, :])
                buf[k, :, s:s + 256] = (buf[k, :, s:s + 256].astype(F32) - (LEARN_RATE * ALPHA_SCALE) * delta).astype(BF16)
            pltpu.make_async_copy(buf.at[k], dst.at[k - base], osem.at[k]).start()
            return carry

        lax.fori_loop(0, per, body, 0)
    for k in range(count):
        dst, at = (nu_hbm, k) if k < 2 * per else (nd_hbm, k - 2 * per)
        pltpu.make_async_copy(buf.at[k], dst.at[at], osem.at[k]).wait()


def call_w(wu, wd, n, p, q):
    part = 456
    per = FF // part
    count = 4 * per
    whole = pl.BlockSpec(memory_space=pltpu.VMEM)
    out = jax.ShapeDtypeStruct((2 * per, part, D), BF16)
    dma = pltpu.SemaphoreType.DMA
    nu, nd = pl.pallas_call(
        functools.partial(kernel_w, count, part),
        in_specs=[ANY, ANY, ANY, whole, whole],
        out_specs=[ANY, ANY],
        out_shape=[out, out],
        scratch_shapes=[pltpu.VMEM((count, part, D), BF16), pltpu.VMEM((count, part, RANK), BF16), dma((count,)), dma((4,)), dma((count,))],
        compiler_params=pltpu.CompilerParams(vmem_limit_bytes=60000000),
        cost_estimate=pl.CostEstimate(flops=6 * 10**9, bytes_accessed=50 * 10**6, transcendentals=0),
        name="pass_w",
    )(wu.reshape(2 * per, part, D), wd.reshape(2 * per, part, D), n.reshape(count, part, RANK), p, q)
    return nu.reshape(2, FF, D), nd.reshape(2, FF, D)


def solution(mesh):
    def local_step(x_loc, dh_loc, w_up, w_down, proj_up, proj_down, mom_up, var_up, mom_down, var_down):
        w_up_t = jnp.swapaxes(w_up, 1, 2)
        pt, qt = jnp.swapaxes(proj_up, 1, 2), jnp.swapaxes(proj_down, 1, 2)
        z0, a0, dz1, u0, rx = call_a(x_loc, dh_loc, pt, qt, w_up_t, w_down)
        g1, sums, ry = call_c(dh_loc, dz1, a0, w_up_t, qt, rx.reshape((2, 2) + CUBE))
        up, down = (2, 0, 1), (1, 0, 2)
        mu, vu, md, vd, dirs = call_d(
            z0, g1, u0, w_down, sums, ry.reshape((2,) + CUBE), jnp.transpose(mom_up, up), jnp.transpose(var_up, up),
            jnp.transpose(mom_down, down), jnp.transpose(var_down, down))
        new_mom_up, new_var_up = jnp.transpose(mu, (1, 2, 0)), jnp.transpose(vu, (1, 2, 0))
        new_mom_down, new_var_down = jnp.transpose(md, (1, 0, 2)), jnp.transpose(vd, (1, 0, 2))
        new_up, new_w_down = call_w(w_up_t, w_down, dirs, proj_up, proj_down)
        return jnp.swapaxes(new_up, 1, 2), new_w_down, new_mom_up, new_var_up, new_mom_down, new_var_down

    tok_spec = P('data', None)
    up_spec = P(None, None, 'data')
    down_spec = P(None, 'data', None)
    return jax.shard_map(
        local_step,
        mesh=mesh,
        in_specs=(tok_spec, tok_spec, P(), P(), P(), P(), up_spec, up_spec, down_spec, down_spec),
        out_specs=(P(), P(), up_spec, up_spec, down_spec, down_spec),
        check_vma=False,
    )
```

time: 309 us -> 314 us (1.016)
  local copies, waits for them, and re-layouts: 2.94 us -> 7.51 us
    pallas_call x2, Pallas kernels: 23.8 us -> 68.8 us  [the longest x1 48.2 us: call_c(): pl.pallas_call(functools.partial(kernel_c, tile, tiles), grid=(tiles,), i...]
    pallas_call x1, Pallas kernels: 182 us -> 139 us  [call_a(): pl.pallas_call(functools.partial(kernel_a, tile, tiles), grid=(tiles,), i...]
    unnamed x12 -> x14, local copies, waits for them, and re-layouts: 2.94 us -> 7.51 us
where the time goes in v1:
time: 314 us
  Pallas kernels  305 us (97%)
  local copies, waits for them, and re-layouts  7.51 us (2%)
    pallas_call x1, Pallas kernels, call_a(): pl.pallas_call(functools.partial(kernel_a, tile, tiles), grid=(tiles,), i...  139 us
    pallas_call x1, Pallas kernels, call_d(): pl.pallas_call(functools.partial(kernel_d, tile, rows // tile, width, chu...  98.1 us
    pallas_call x1, Pallas kernels, call_c(): pl.pallas_call(functools.partial(kernel_c, tile, tiles), grid=(tiles,), i...  48.2 us
    pallas_call x1, Pallas kernels, call_w(): pl.pallas_call(functools.partial(kernel_w, count, part), in_specs=[ANY, A...  20.6 us
    unnamed x14, local copies, waits for them, and re-layouts  7.51 us

profile of v1, /device:TPU:0, one launch (start us, length us, event | category | flops | bytes accessed | tf_op | source)
XLA Modules:
  0.0 313.7 jit_solution(8983549236976722581)
XLA Ops:
  0.6 2.3 copy.16
  2.9 2.3 copy.17
  5.2 138.5 %pass_a.1 = (f32[4096,2736]{1,0:T(8,128)}, bf16[4096,2736]{1,0:T(8,128)(2,1)}, bf16[4096,2736]{1,0:T(8,128)(2,1)}, bf16[256,4096]{1,0:T(8,128)(2,1)}, f32[2,16,176,256]{3,2,1,0:T(8,128)}) custom-call(bf16[4096,1024]{1,0:T(8,128)(2,1)} %x_ref.1, bf16[4096,1024]{1,0:T(8,128)(2,1)} %dh_ref.3, bf16[2,256,1024]{2,1,0:T(8,128)(2,1)} %bitcast.28, ...), custom_call_target="tpu_custom_call" | custom-call | flops 109999996928 | bytes 140000000 | tf_op jit(solution)/shard_map/pass_a/pallas_call | solution.py:173
  143.7 48.2 %pass_c.1 = (bf16[4096,1024]{1,0:T(8,128)(2,1)}, f32[2,176,256]{2,1,0:T(8,128)}, f32[16,176,256]{2,1,0:T(8,128)}) custom-call(bf16[4096,1024]{1,0:T(8,128)(2,1)} %dh_ref.3, bf16[4096,2736]{1,0:T(8,128)(2,1)} %get-tuple-element.22.dz_ref, bf16[4096,2736]{1,0:T(8,128)(2,1)} %get-tuple-element.23.a0_ref, bf16[2,2736,1024]{2,1,0:T(8,128)(2,1)} %bitcast.22, ...), custom_call_target="tpu_custom_call" | custom-call | flops 31000000512 | bytes 70000000 | tf_op jit(solution)/shard_map/pass_c/pallas_call | solution.py:350
  192.0 98.1 %pass_d.1 = (f32[171,2,256]{2,1,0:T(2,128)}, f32[171,2,256]{2,1,0:T(2,128)}, f32[171,2,256]{2,1,0:T(2,128)}, f32[171,2,256]{2,1,0:T(2,128)}, bf16[4,2736,256]{2,1,0:T(8,128)(2,1)}) custom-call(f32[4096,2736]{1,0:T(8,128)} %get-tuple-element.21.z0_ref, bf16[2,2736,1024]{2,1,0:T(8,128)(2,1)} %w2_ref.1, f32[2,176,256]{2,1,0:T(8,128)} %get-tuple-element.25.sum_ref, ...), custom_call_target="tpu_custom_call" | custom-call | flops 30000001024 | bytes 70000000 | tf_op jit(solution)/shard_map/pass_d/pallas_call | solution.py:520
  290.1 0.0 copy-start.3
  290.1 0.0 copy-start.2
  290.1 0.0 copy-start.1
  290.1 0.0 copy-start
  290.1 20.6 %pass_w.1 = (bf16[12,456,1024]{2,1,0:T(8,128)(2,1)}, bf16[12,456,1024]{2,1,0:T(8,128)(2,1)}) custom-call(bf16[12,456,1024]{2,1,0:T(8,128)(2,1)} %bitcast.23, bf16[12,456,1024]{2,1,0:T(8,128)(2,1)} %bitcast.24, bf16[24,456,256]{2,1,0:T(8,128)(2,1)} %bitcast.25, bf16[2,1024,256]{2,1,0:T(8,128)(2,1)} %p_ref.1, bf16[2,1024,256]{2,1,0:T(8,128)(2,1)} %q_ref.1), custom_call_target="tpu_custom_call" | custom-call | flops 6000000000 | bytes 50000000 | tf_op jit(solution)/shard_map/pass_w/pallas_call | solution.py:586
  310.7 0.0 copy-done.3
  310.7 0.7 copy.22
  311.5 0.0 copy-done.2
  311.5 0.7 copy.23
  312.2 0.0 copy-done.1
  312.2 0.7 copy.24
  313.0 0.0 copy-done
  313.0 0.7 copy.25
Async XLA Ops:
  290.1 20.6 %copy-start.3 = (f32[171,2,256]{2,1,0:T(2,128)S(1)}, f32[171,2,256]{2,1,0:T(2,128)}, u32[]{:S(2)}) copy-start(f32[171,2,256]{2,1,0:T(2,128)} %get-tuple-element.32) | copy-start | bytes 1050628
  290.1 21.4 %copy-start.2 = (f32[171,2,256]{2,1,0:T(2,128)S(1)}, f32[171,2,256]{2,1,0:T(2,128)}, u32[]{:S(2)}) copy-start(f32[171,2,256]{2,1,0:T(2,128)} %get-tuple-element.33) | copy-start | bytes 1050628
  290.1 22.1 %copy-start.1 = (f32[171,2,256]{2,1,0:T(2,128)S(1)}, f32[171,2,256]{2,1,0:T(2,128)}, u32[]{:S(2)}) copy-start(f32[171,2,256]{2,1,0:T(2,128)} %get-tuple-element.34) | copy-start | bytes 1050628
  290.1 22.8 %copy-start = (f32[171,2,256]{2,1,0:T(2,128)S(1)}, f32[171,2,256]{2,1,0:T(2,128)}, u32[]{:S(2)}) copy-start(f32[171,2,256]{2,1,0:T(2,128)} %get-tuple-element.35) | copy-start | bytes 1050628

commit v2 on v1

--- a/solution.py
+++ b/solution.py
@@ -31,6 +31,11 @@
     return [(s, min(width, FF - s)) for s in range(0, FF, width)]
 
 
+def pieces(span, width=256):
+    s, w = span
+    return [(t, min(width, s + w - t)) for t in range(s, s + w, width)]
+
+
 def dot_nn(a, b):
     return lax.dot_general(a, b, (((1,), (0,)), ((), ())), preferred_element_type=F32)
 
@@ -39,10 +44,8 @@
     return lax.dot_general(a, b, (((1,), (1,)), ((), ())), preferred_element_type=F32)
 
 
-def gelu_val(z):
-    z2 = z * z
-    t = jnp.tanh(z * (C0 + C1 * z2))
-    return z * (0.5 * t + 0.5)
+def dot_tt(a, b):
+    return lax.dot_general(a, b, (((0,), (1,)), ((), ())), preferred_element_type=F32)
 
 
 def gelu_both(z):
@@ -59,8 +62,8 @@
 
 
 def kernel_a(tile, tiles, x_ref, dh_ref, p_ref, q_ref, w1_hbm, w2_hbm,
-             z0_hbm, a0_hbm, dz1, u0_ref, r_hbm,
-             w1a, w2a, w1b, w2b, z0, a0, h1, zs, das, ac, u1, v1, r1, r2, blk, sem, zsem):
+             slope_hbm, a0_hbm, dz1, u0_ref, r_hbm,
+             w1a, w2a, w1b, w2b, slope, a0, h1, zs, das, ac, u1, v1, r1, r2, blk, sem, zsem):
     i = pl.program_id(0)
     width, slab = 512, 16
     spans = spans_of(width)
@@ -72,7 +75,7 @@
     ]
 
     def out(idx, k):
-        src, dst = ((z0, z0_hbm), (a0, a0_hbm))[k]
+        src, dst = ((slope, slope_hbm), (a0, a0_hbm))[k]
         return pltpu.make_async_copy(src, dst.at[pl.ds(pl.multiple_of(idx * tile, tile), tile)], zsem.at[k])
 
     @pl.when(i == 0)
@@ -92,21 +95,24 @@
     x = x_ref[...]
     dh = dh_ref[...]
 
-    def act0(span):
-        s, w = span
-        for r in range(0, tile, slab):
-            a0[r:r + slab, s:s + w] = gelu_val(z0[r:r + slab, s:s + w]).astype(BF16)
-
-    prev = None
-    for span in spans:
-        s, w = span
-        z0[:, s:s + w] = dot_nt(x, w1a[s:s + w, :])
-        if prev is not None:
-            act0(prev)
-        prev = span
-    u0_ref[...] = dot_nt(p_ref[0], x).astype(BF16)
-    v1[...] = dot_nt(q_ref[1], dh).astype(BF16)
-    act0(prev)
+    def act0(span, k):
+        for s, w in pieces(span):
+            o = s - span[0]
+            for r in range(0, tile, slab):
+                a, g = gelu_both(zs[k, r:r + slab, o:o + w])
+                a0[r:r + slab, s:s + w] = a.astype(BF16)
+                slope[r:r + slab, s:s + w] = g
+
+    n = len(spans)
+    for j in range(n + 1):
+        if j < n:
+            s, w = spans[j]
+            zs[j % 2, :, :w] = dot_nt(x, w1a[s:s + w, :])
+        else:
+            u0_ref[...] = dot_tt(p_ref[0], x).astype(BF16)
+            v1[...] = dot_tt(q_ref[1], dh).astype(BF16)
+        if j > 0:
+            act0(spans[j - 1], (j - 1) % 2)
 
     for n in range(0, D, width):
         h1[:, n:n + width] = (x_ref[:, n:n + width].astype(F32) + dot_nn(a0[...], w2a[:, n:n + width])).astype(BF16)
@@ -114,11 +120,12 @@
     out(i, 1).start()
 
     def act1(span, k):
-        s, w = span
-        for r in range(0, tile, slab):
-            a, g = gelu_both(zs[k, r:r + slab, :w])
-            ac[k, r:r + slab, :w] = a.astype(BF16)
-            dz1[r:r + slab, s:s + w] = (g * das[k, r:r + slab, :w]).astype(BF16)
+        for s, w in pieces(span):
+            o = s - span[0]
+            for r in range(0, tile, slab):
+                a, g = gelu_both(zs[k, r:r + slab, o:o + w])
+                ac[k, r:r + slab, o:o + w] = a.astype(BF16)
+                dz1[r:r + slab, s:s + w] = (g * das[k, r:r + slab, o:o + w]).astype(BF16)
 
     def acc1(span, k):
         s, w = span
@@ -133,7 +140,7 @@
             das[j % 2, :, :w] = dot_nt(dh, w2b[s:s + w, :])
             zs[j % 2, :, :w] = dot_nt(h, w1b[s:s + w, :])
         if j == 0:
-            u1[...] = dot_nt(p_ref[1], h).astype(BF16)
+            u1[...] = dot_tt(p_ref[1], h).astype(BF16)
         if 1 <= j <= n:
             act1(spans[j - 1], (j - 1) % 2)
         if j >= 2:
@@ -145,7 +152,7 @@
         out(i, 1).wait()
         for k, acc in enumerate((r1, r2)):
             for t in range(FFP // 256):
-                z0[t % 2 * 256:t % 2 * 256 + 256, t // 2 * 256:t // 2 * 256 + 256] = acc[:, t * 256:t * 256 + 256].T
+                slope[t % 2 * 256:t % 2 * 256 + 256, t // 2 * 256:t // 2 * 256 + 256] = acc[:, t * 256:t * 256 + 256].T
             if k == 1:
                 pltpu.make_async_copy(blk, r_hbm.at[0], sem.at[0]).wait()
             for d in range(DEV):
@@ -154,7 +161,7 @@
                     t, lo = row // 256, row % 256
                     take = min(end - row, 256 - lo)
                     to = row - SHARD * d
-                    blk[(d % 2) * 8 + d // 2, to:to + take, :] = z0[t % 2 * 256 + lo:t % 2 * 256 + lo + take, t // 2 * 256:t // 2 * 256 + 256]
+                    blk[(d % 2) * 8 + d // 2, to:to + take, :] = slope[t % 2 * 256 + lo:t % 2 * 256 + lo + take, t // 2 * 256:t // 2 * 256 + 256]
                     row += take
             pltpu.make_async_copy(blk, r_hbm.at[k], sem.at[k]).start()
         pltpu.make_async_copy(blk, r_hbm.at[1], sem.at[1]).wait()
@@ -168,7 +175,7 @@
 def call_a(x, dh, p, q, w1, w2):
     rows, tile = x.shape[0], 512
     tiles = rows // tile
-    whole = pl.BlockSpec((2, RANK, D), lambda i: (0, 0, 0), pipeline_mode=ONCE)
+    whole = pl.BlockSpec((2, D, RANK), lambda i: (0, 0, 0), pipeline_mode=ONCE)
     rowspec = pl.BlockSpec((tile, D), lambda i: (i, 0))
     return pl.pallas_call(
         functools.partial(kernel_a, tile, tiles),
@@ -208,9 +215,11 @@
     return new_mom, new_var, direction
 
 
+AHEAD = 10
 AXES = ((2, 1, 0), (1, 0, 2), (0, 2, 1))
-RS_ROWS = ((0, 56), (56, 56), (112, 64))
-AG_ROWS = ((0, 48), (48, 64), (112, 64))
+RS_ROWS = ((0, 56), (56, 56), (112, 64), (0, 24), (56, 24), (112, 32), (24, 32), (80, 32), (144, 32))
+AG_ROWS = ((0, 48), (48, 64), (112, 64), (0, 16), (48, 32), (112, 32), (16, 32), (80, 32), (144, 32))
+THIRDS, SIXTHS = range(3), range(3, 9)
 MESH = pl.DeviceIdType.MESH
 CUBE = (2, 2, 2, PAD, RANK)
 
@@ -240,7 +249,7 @@
 
     def rs_copy(self, flow, stage):
         own, other, bufs, sems, p = flow
-        rows, axes = RS_ROWS[p], AXES[p]
+        rows, axes = RS_ROWS[p], AXES[p % 3]
         s, r = (sem.at[p, stage] for sem in sems)
         if stage == 0:
             spot = view({}, rows)
@@ -253,7 +262,7 @@
 
     def rs_step(self, flow, stage):
         own, _, bufs, _, p = flow
-        rows, axes = RS_ROWS[p], AXES[p]
+        rows, axes = RS_ROWS[p], AXES[p % 3]
         self.rs_copy(flow, stage).wait()
         ref = own.at[view({a: self.bits[a] for a in axes[:stage]}, rows)]
         ref[...] = ref[...] + bufs[stage][(slice(None),) * (3 - stage) + (pl.ds(*rows), slice(None))]
@@ -261,7 +270,7 @@
             self.rs_copy(flow, stage + 1).start()
 
     def ag_copy(self, gat, sems, kind, p, slot):
-        rows, axes, bits = AG_ROWS[p], AXES[p], self.bits
+        rows, axes, bits = AG_ROWS[p], AXES[p % 3], self.bits
         if slot == 0:
             at, axis = {a: bits[a] for a in range(3)}, 3
         elif slot <= 3:
@@ -325,7 +334,7 @@
     half = 512
     for n in range(0, D, half):
         g1_ref[:, n:n + half] = (dh_ref[:, n:n + half].astype(F32) + dot_nn(dz_ref[...], w1_ref[:, n:n + half])).astype(BF16)
-    v0 = dot_nt(q_ref[...], g1_ref[...]).astype(BF16)
+    v0 = dot_tt(q_ref[...], g1_ref[...]).astype(BF16)
     for s, w in spans_of(512):
         r3[:, s:s + w] += dot_nn(v0, a0_ref[:, s:s + w])
 
@@ -355,7 +364,7 @@
             pl.BlockSpec((tile, FF), lambda i: (i, 0)),
             pl.BlockSpec((tile, FF), lambda i: (i, 0)),
             pl.BlockSpec((None, FF, D), lambda i: (1, 0, 0), pipeline_mode=ONCE),
-            pl.BlockSpec((None, RANK, D), lambda i: (0, 0, 0), pipeline_mode=ONCE),
+            pl.BlockSpec((None, D, RANK), lambda i: (0, 0, 0), pipeline_mode=ONCE),
             ANY,
         ],
         out_specs=[
@@ -381,7 +390,7 @@
 
 
 def kernel_d(tile, tiles, width, chunks,
-             z0_ref, w2_ref, sum_ref, mu, vu, md, vd, g1_hbm, u0_hbm, rx_hbm,
+             slope_ref, w2_ref, sum_ref, mu, vu, md, vd, g1_hbm, u0_hbm, rx_hbm,
              mu_o, vu_o, md_o, vd_o, n_hbm,
              g1, u0, das, dz, acc_s, racc, rt, own_x, own_y,
              x0, x1, x2, x3, y0, y1, y2, y3, gat, tmp, nb,
@@ -392,7 +401,7 @@
     bits, core = c.bits, c.core
     ag_sems = (ag_s, ag_r)
     flows_x = [(own_x, rx_hbm.at[1 - core], (x0, x1, x2, x3), (rx_s, rx_r), p) for p in range(3)]
-    flows_y = [(own_y.at[core], own_y.at[1 - core], (y0, y1, y2, y3), (ry_s, ry_r), p) for p in range(3)]
+    flows_y = [(own_y.at[core], own_y.at[1 - core], (y0, y1, y2, y3), (ry_s, ry_r), p) for p in SIXTHS]
 
     def rs(flows, stage):
         for flow in flows:
@@ -400,7 +409,7 @@
 
     def ag(kinds, stage):
         for kind in kinds:
-            for p in range(3):
+            for p in SIXTHS if kind == 0 else THIRDS:
                 if stage == 0:
                     c.ag_begin(gat, ag_sems, kind, p)
                 elif stage < 4:
@@ -466,7 +475,7 @@
     def act(t):
         k = t % 2
         for r in range(0, tile, slab):
-            slope = gelu_both(z0_ref[t * tile + r:t * tile + r + slab, :])[1]
+            slope = slope_ref[t * tile + r:t * tile + r + slab, :]
             dz[k, r:r + slab, :] = (slope * das[k, r:r + slab, :]).astype(BF16)
 
     def acc(t):
@@ -534,7 +543,7 @@
             pltpu.VMEM((RANK, width), F32), pltpu.VMEM((2, RANK, width), F32), pltpu.VMEM((FFP, RANK), F32),
             pltpu.VMEM(CUBE, F32), pltpu.VMEM((2,) + CUBE, F32), *stages(), *stages(),
             pltpu.VMEM((4, 2) + CUBE, BF16), pltpu.VMEM((FF, RANK), F32), pltpu.VMEM((2, FF, RANK), BF16),
-            dma((3,)), dma((3, 4)), dma((3, 4)), dma((3, 4)), dma((3, 4)), dma((4, 3, 7)), dma((4, 3, 7)), dma((4,)),
+            dma((3,)), dma((3, 4)), dma((3, 4)), dma((9, 4)), dma((9, 4)), dma((4, 9, 7)), dma((4, 9, 7)), dma((4,)),
         ],
         compiler_params=pltpu.CompilerParams(
             dimension_semantics=("arbitrary",), collective_id=0, has_side_effects=True, vmem_limit_bytes=67000000),
@@ -553,10 +562,12 @@
     def names(kind):
         return pltpu.make_async_copy(n_hbm.at[pl.ds(kind * per, per)], n.at[pl.ds(kind * per, per)], nsem.at[kind])
 
+    ahead = AHEAD
     for k in range(count):
         if k % per == 0:
             names(k // per).start()
-        load(k).start()
+        if k < ahead:
+            load(k).start()
     for kind in range(4):
         proj, dst, base = (p_ref, nu_hbm, 0) if kind < 2 else (q_ref, nd_hbm, 2 * per)
         names(kind).wait()
@@ -564,6 +575,16 @@
         def body(t, carry):
             k = kind * per + t
             pltpu.make_async_copy(wu_hbm.at[0], buf.at[k], isem.at[k]).wait()
+            more = k + ahead
+
+            @pl.when(more < 2 * per)
+            def _():
+                pltpu.make_async_copy(wu_hbm.at[more], buf.at[more], isem.at[more]).start()
+
+            @pl.when(jnp.logical_and(more >= 2 * per, more < count))
+            def _():
+                pltpu.make_async_copy(wd_hbm.at[more - 2 * per], buf.at[more], isem.at[more]).start()
+
             for s in range(0, D, 256):
                 delta = dot_nt(n[k], proj[kind % 2, s:s + 256, :])
                 buf[k, :, s:s + 256] = (buf[k, :, s:s + 256].astype(F32) - (LEARN_RATE * ALPHA_SCALE) * delta).astype(BF16)
@@ -599,9 +620,8 @@
 def solution(mesh):
     def local_step(x_loc, dh_loc, w_up, w_down, proj_up, proj_down, mom_up, var_up, mom_down, var_down):
         w_up_t = jnp.swapaxes(w_up, 1, 2)
-        pt, qt = jnp.swapaxes(proj_up, 1, 2), jnp.swapaxes(proj_down, 1, 2)
-        z0, a0, dz1, u0, rx = call_a(x_loc, dh_loc, pt, qt, w_up_t, w_down)
-        g1, sums, ry = call_c(dh_loc, dz1, a0, w_up_t, qt, rx.reshape((2, 2) + CUBE))
+        z0, a0, dz1, u0, rx = call_a(x_loc, dh_loc, proj_up, proj_down, w_up_t, w_down)
+        g1, sums, ry = call_c(dh_loc, dz1, a0, w_up_t, proj_down, rx.reshape((2, 2) + CUBE))
         up, down = (2, 0, 1), (1, 0, 2)
         mu, vu, md, vd, dirs = call_d(
             z0, g1, u0, w_down, sums, ry.reshape((2,) + CUBE), jnp.transpose(mom_up, up), jnp.transpose(var_up, up),

time: 314 us -> 305 us (0.971)
  local copies, waits for them, and re-layouts: 7.51 us -> 2.95 us
  Pallas kernels: 305 us -> 301 us
    pallas_call x1, Pallas kernels: 98.1 us -> 90.4 us  [call_d(): pl.pallas_call(functools.partial(kernel_d, tile, rows // tile, width, chu...]
    pallas_call x1, Pallas kernels: 139 us -> 144 us  [call_a(): pl.pallas_call(functools.partial(kernel_a, tile, tiles), grid=(tiles,), i...]
    unnamed x14 -> x12, local copies, waits for them, and re-layouts: 7.51 us -> 2.95 us
where the time goes in v2:
time: 305 us
  Pallas kernels  301 us (99%)
    pallas_call x1, Pallas kernels, call_a(): pl.pallas_call(functools.partial(kernel_a, tile, tiles), grid=(tiles,), i...  144 us
    pallas_call x1, Pallas kernels, call_d(): pl.pallas_call(functools.partial(kernel_d, tile, rows // tile, width, chu...  90.4 us
    pallas_call x1, Pallas kernels, call_c(): pl.pallas_call(functools.partial(kernel_c, tile, tiles), grid=(tiles,), i...  48.2 us
    pallas_call x1, Pallas kernels, call_w(): pl.pallas_call(functools.partial(kernel_w, count, part), in_specs=[ANY, A...  19 us

profile of v2, /device:TPU:0, one launch (start us, length us, event | category | flops | bytes accessed | tf_op | source)
XLA Modules:
  0.0 304.9 jit_solution(5135508327581191274)
XLA Ops:
  0.6 143.6 %pass_a.1 = (f32[4096,2736]{1,0:T(8,128)}, bf16[4096,2736]{1,0:T(8,128)(2,1)}, bf16[4096,2736]{1,0:T(8,128)(2,1)}, bf16[256,4096]{1,0:T(8,128)(2,1)}, f32[2,16,176,256]{3,2,1,0:T(8,128)}) custom-call(bf16[4096,1024]{1,0:T(8,128)(2,1)} %x_ref.1, bf16[4096,1024]{1,0:T(8,128)(2,1)} %dh_ref.3, bf16[2,1024,256]{2,1,0:T(8,128)(2,1)} %p_ref.3, ...), custom_call_target="tpu_custom_call" | custom-call | flops 109999996928 | bytes 140000000 | tf_op jit(solution)/shard_map/pass_a/pallas_call | solution.py:180
  144.2 48.2 %pass_c.1 = (bf16[4096,1024]{1,0:T(8,128)(2,1)}, f32[2,176,256]{2,1,0:T(8,128)}, f32[16,176,256]{2,1,0:T(8,128)}) custom-call(bf16[4096,1024]{1,0:T(8,128)(2,1)} %dh_ref.3, bf16[4096,2736]{1,0:T(8,128)(2,1)} %get-tuple-element.22.dz_ref, bf16[4096,2736]{1,0:T(8,128)(2,1)} %get-tuple-element.23.a0_ref, bf16[2,2736,1024]{2,1,0:T(8,128)(2,1)} %bitcast.20, ...), custom_call_target="tpu_custom_call" | custom-call | flops 31000000512 | bytes 70000000 | tf_op jit(solution)/shard_map/pass_c/pallas_call | solution.py:359
  192.5 90.4 %pass_d.1 = (f32[171,2,256]{2,1,0:T(2,128)}, f32[171,2,256]{2,1,0:T(2,128)}, f32[171,2,256]{2,1,0:T(2,128)}, f32[171,2,256]{2,1,0:T(2,128)}, bf16[4,2736,256]{2,1,0:T(8,128)(2,1)}) custom-call(f32[4096,2736]{1,0:T(8,128)} %get-tuple-element.21.slope_ref, bf16[2,2736,1024]{2,1,0:T(8,128)(2,1)} %w2_ref.1, f32[2,176,256]{2,1,0:T(8,128)} %get-tuple-element.25.sum_ref, ...), custom_call_target="tpu_custom_call" | custom-call | flops 30000001024 | bytes 70000000 | tf_op jit(solution)/shard_map/pass_d/pallas_call | solution.py:529
  282.9 0.0 copy-start.3
  282.9 0.0 copy-start.2
  282.9 0.0 copy-start.1
  282.9 0.0 copy-start
  282.9 19.0 %pass_w.1 = (bf16[12,456,1024]{2,1,0:T(8,128)(2,1)}, bf16[12,456,1024]{2,1,0:T(8,128)(2,1)}) custom-call(bf16[12,456,1024]{2,1,0:T(8,128)(2,1)} %bitcast.21, bf16[12,456,1024]{2,1,0:T(8,128)(2,1)} %bitcast.22, bf16[24,456,256]{2,1,0:T(8,128)(2,1)} %bitcast.23, bf16[2,1024,256]{2,1,0:T(8,128)(2,1)} %p_ref.3, bf16[2,1024,256]{2,1,0:T(8,128)(2,1)} %q_ref.5), custom_call_target="tpu_custom_call" | custom-call | flops 6000000000 | bytes 50000000 | tf_op jit(solution)/shard_map/pass_w/pallas_call | solution.py:607
  301.9 0.0 copy-done.3
  301.9 0.7 copy.20
  302.6 0.0 copy-done.2
  302.6 0.7 copy.21
  303.4 0.0 copy-done.1
  303.4 0.7 copy.22
  304.1 0.0 copy-done
  304.1 0.7 copy.23
Async XLA Ops:
  282.9 19.0 %copy-start.3 = (f32[171,2,256]{2,1,0:T(2,128)S(1)}, f32[171,2,256]{2,1,0:T(2,128)}, u32[]{:S(2)}) copy-start(f32[171,2,256]{2,1,0:T(2,128)} %get-tuple-element.32) | copy-start | bytes 1050628
  282.9 19.8 %copy-start.2 = (f32[171,2,256]{2,1,0:T(2,128)S(1)}, f32[171,2,256]{2,1,0:T(2,128)}, u32[]{:S(2)}) copy-start(f32[171,2,256]{2,1,0:T(2,128)} %get-tuple-element.33) | copy-start | bytes 1050628
  282.9 20.5 %copy-start.1 = (f32[171,2,256]{2,1,0:T(2,128)S(1)}, f32[171,2,256]{2,1,0:T(2,128)}, u32[]{:S(2)}) copy-start(f32[171,2,256]{2,1,0:T(2,128)} %get-tuple-element.34) | copy-start | bytes 1050628
  282.9 21.2 %copy-start = (f32[171,2,256]{2,1,0:T(2,128)S(1)}, f32[171,2,256]{2,1,0:T(2,128)}, u32[]{:S(2)}) copy-start(f32[171,2,256]{2,1,0:T(2,128)} %get-tuple-element.35) | copy-start | bytes 1050628

commit v3 on v2

--- a/solution.py
+++ b/solution.py
@@ -62,8 +62,8 @@
 
 
 def kernel_a(tile, tiles, x_ref, dh_ref, p_ref, q_ref, w1_hbm, w2_hbm,
-             slope_hbm, a0_hbm, dz1, u0_ref, r_hbm,
-             w1a, w2a, w1b, w2b, slope, a0, h1, zs, das, ac, u1, v1, r1, r2, blk, sem, zsem):
+             slope_hbm, g1_hbm, u0_ref, r_hbm,
+             w1a, w2a, w1b, w2b, slope, a0, h1, dz1, zs, das, ac, u1, v1, r1, r2, r3, blk, sem, zsem):
     i = pl.program_id(0)
     width, slab = 512, 16
     spans = spans_of(width)
@@ -74,9 +74,16 @@
         pltpu.make_async_copy(w2_hbm.at[1], w2b, sem.at[3]),
     ]
 
+    chunks = FFP // 256
+
     def out(idx, k):
-        src, dst = ((slope, slope_hbm), (a0, a0_hbm))[k]
-        return pltpu.make_async_copy(src, dst.at[pl.ds(pl.multiple_of(idx * tile, tile), tile)], zsem.at[k])
+        rows = pl.ds(pl.multiple_of(idx * tile, tile), tile)
+        if k == chunks:
+            return pltpu.make_async_copy(h1, g1_hbm.at[rows], zsem.at[k])
+        return pltpu.make_async_copy(slope.at[:, k * 256:k * 256 + 256], slope_hbm.at[k, rows], zsem.at[k])
+
+    def outs(idx):
+        return [out(idx, k) for k in range(chunks + 1)]
 
     @pl.when(i == 0)
     def _():
@@ -84,13 +91,14 @@
             cp.start()
         r1[...] = jnp.zeros_like(r1)
         r2[...] = jnp.zeros_like(r2)
+        r3[...] = jnp.zeros_like(r3)
         for cp in loads:
             cp.wait()
 
     @pl.when(i > 0)
     def _():
-        out(i - 1, 0).wait()
-        out(i - 1, 1).wait()
+        for cp in outs(i - 1):
+            cp.wait()
 
     x = x_ref[...]
     dh = dh_ref[...]
@@ -116,8 +124,8 @@
 
     for n in range(0, D, width):
         h1[:, n:n + width] = (x_ref[:, n:n + width].astype(F32) + dot_nn(a0[...], w2a[:, n:n + width])).astype(BF16)
-    out(i, 0).start()
-    out(i, 1).start()
+    for k in range(chunks):
+        out(i, k).start()
 
     def act1(span, k):
         for s, w in pieces(span):
@@ -146,15 +154,22 @@
         if j >= 2:
             acc1(spans[j - 2], (j - 2) % 2)
 
+    for n in range(0, D, width):
+        h1[:, n:n + width] = (dh_ref[:, n:n + width].astype(F32) + dot_nn(dz1[...], w1b[:, n:n + width])).astype(BF16)
+    v0 = dot_tt(q_ref[0], h1[...]).astype(BF16)
+    out(i, chunks).start()
+    for s, w in spans:
+        r3[:, s:s + w] += dot_nn(v0, a0[:, s:s + w])
+
     @pl.when(i == tiles - 1)
     def _():
-        out(i, 0).wait()
-        out(i, 1).wait()
-        for k, acc in enumerate((r1, r2)):
+        for cp in outs(i):
+            cp.wait()
+        for k, acc in enumerate((r1, r2, r3)):
             for t in range(FFP // 256):
                 slope[t % 2 * 256:t % 2 * 256 + 256, t // 2 * 256:t // 2 * 256 + 256] = acc[:, t * 256:t * 256 + 256].T
-            if k == 1:
-                pltpu.make_async_copy(blk, r_hbm.at[0], sem.at[0]).wait()
+            if k > 0:
+                pltpu.make_async_copy(blk, r_hbm.at[k - 1], sem.at[k - 1]).wait()
             for d in range(DEV):
                 row, end = SHARD * d, SHARD * d + PAD
                 while row < end:
@@ -164,12 +179,7 @@
                     blk[(d % 2) * 8 + d // 2, to:to + take, :] = slope[t % 2 * 256 + lo:t % 2 * 256 + lo + take, t // 2 * 256:t // 2 * 256 + 256]
                     row += take
             pltpu.make_async_copy(blk, r_hbm.at[k], sem.at[k]).start()
-        pltpu.make_async_copy(blk, r_hbm.at[1], sem.at[1]).wait()
-
-
-def leave(acc, rt):
-    for s in range(0, FFP, 256):
-        rt[s:s + 256, :] = acc[:, s:s + 256].T
+        pltpu.make_async_copy(blk, r_hbm.at[2], sem.at[2]).wait()
 
 
 def call_a(x, dh, p, q, w1, w2):
@@ -181,23 +191,22 @@
         functools.partial(kernel_a, tile, tiles),
         grid=(tiles,),
         in_specs=[rowspec, rowspec, whole, whole, ANY, ANY],
-        out_specs=[ANY, ANY, pl.BlockSpec((tile, FF), lambda i: (i, 0)), pl.BlockSpec((RANK, tile), lambda i: (0, i)), ANY],
+        out_specs=[ANY, ANY, pl.BlockSpec((RANK, tile), lambda i: (0, i)), ANY],
         out_shape=[
-            jax.ShapeDtypeStruct((rows, FF), F32),
-            jax.ShapeDtypeStruct((rows, FF), BF16),
-            jax.ShapeDtypeStruct((rows, FF), BF16),
+            jax.ShapeDtypeStruct((FFP // 256, rows, 256), F32),
+            jax.ShapeDtypeStruct((rows, D), BF16),
             jax.ShapeDtypeStruct((RANK, rows), BF16),
-            jax.ShapeDtypeStruct((2, DEV, PAD, RANK), F32),
+            jax.ShapeDtypeStruct((3, DEV, PAD, RANK), F32),
         ],
         scratch_shapes=[
             pltpu.VMEM((FF, D), BF16), pltpu.VMEM((FF, D), BF16),
             pltpu.VMEM((FF, D), BF16), pltpu.VMEM((FF, D), BF16),
-            pltpu.VMEM((tile, FF), F32), pltpu.VMEM((tile, FF), BF16), pltpu.VMEM((tile, D), BF16),
+            pltpu.VMEM((tile, FFP), F32), pltpu.VMEM((tile, FF), BF16), pltpu.VMEM((tile, D), BF16), pltpu.VMEM((tile, FF), BF16),
             pltpu.VMEM((2, tile, 512), F32), pltpu.VMEM((2, tile, 512), F32), pltpu.VMEM((2, tile, 512), BF16),
             pltpu.VMEM((RANK, tile), BF16), pltpu.VMEM((RANK, tile), BF16),
-            pltpu.VMEM((RANK, FFP), F32), pltpu.VMEM((RANK, FFP), F32),
+            pltpu.VMEM((RANK, FFP), F32), pltpu.VMEM((RANK, FFP), F32), pltpu.VMEM((RANK, FFP), F32),
             pltpu.VMEM((DEV, PAD, RANK), F32),
-            pltpu.SemaphoreType.DMA((4,)), pltpu.SemaphoreType.DMA((2,)),
+            pltpu.SemaphoreType.DMA((4,)), pltpu.SemaphoreType.DMA((FFP // 256 + 1,)),
         ],
         compiler_params=pltpu.CompilerParams(
             dimension_semantics=("arbitrary",), vmem_limit_bytes=67000000),
@@ -300,107 +309,21 @@
     return [pltpu.VMEM(CUBE[k:], F32) if k else pltpu.VMEM(CUBE, F32) for k in range(4)]
 
 
-def kernel_c(tile, tiles, dh_ref, dz_ref, a0_ref, w1_ref, q_ref, rx_hbm,
-             g1_ref, sum_ref, ry_hbm,
-             r3, rt, blk, own, xa0, xa1, xa2, xa3, xb0, xb1, xb2, xb3, lsem, as_, ar, bs, br):
-    i = pl.program_id(0)
-    c = Comm()
-    bufs = ((xa0, xa1, xa2, xa3), (xb0, xb1, xb2, xb3))
-    sems = ((as_, ar), (bs, br))
-    flows = [(own.at[k], rx_hbm.at[k, 1 - c.core], bufs[k], sems[k], p) for k in range(2) for p in range(3)]
-
-    def mine():
-        return pltpu.make_async_copy(rx_hbm.at[:, c.core], own, lsem.at[0])
-
-    @pl.when(i == 0)
-    def _():
-        c.greet()
-        mine().start()
-        r3[...] = jnp.zeros_like(r3)
-        c.met()
-        for flow in flows:
-            c.rs_copy(flow, 0).start()
-
-    @pl.when(i == 2)
-    def _():
-        mine().wait()
-
-    for at, stage in ((2, 0), (5, 1), (7, 2)):
-        @pl.when(i == at)
-        def _():
-            for flow in flows:
-                c.rs_step(flow, stage)
-
-    half = 512
-    for n in range(0, D, half):
-        g1_ref[:, n:n + half] = (dh_ref[:, n:n + half].astype(F32) + dot_nn(dz_ref[...], w1_ref[:, n:n + half])).astype(BF16)
-    v0 = dot_tt(q_ref[...], g1_ref[...]).astype(BF16)
-    for s, w in spans_of(512):
-        r3[:, s:s + w] += dot_nn(v0, a0_ref[:, s:s + w])
-
-    @pl.when(i == tiles - 1)
-    def _():
-        leave(r3, rt)
-        for d in range(DEV):
-            blk[(d % 2) * 8 + d // 2] = rt[SHARD * d:SHARD * d + PAD, :]
-        out = pltpu.make_async_copy(blk, ry_hbm, lsem.at[0])
-        out.start()
-        for flow in flows:
-            c.rs_step(flow, 3)
-        for k in range(2):
-            sum_ref[k] = own[k, c.bits[0], c.bits[1], c.bits[2]]
-        out.wait()
-
-
-def call_c(dh, dz, a0, w1, q, rx):
-    rows, tile = dh.shape[0], 512
-    tiles = rows // tile
-    dma = pltpu.SemaphoreType.DMA
-    return pl.pallas_call(
-        functools.partial(kernel_c, tile, tiles),
-        grid=(tiles,),
-        in_specs=[
-            pl.BlockSpec((tile, D), lambda i: (i, 0)),
-            pl.BlockSpec((tile, FF), lambda i: (i, 0)),
-            pl.BlockSpec((tile, FF), lambda i: (i, 0)),
-            pl.BlockSpec((None, FF, D), lambda i: (1, 0, 0), pipeline_mode=ONCE),
-            pl.BlockSpec((None, D, RANK), lambda i: (0, 0, 0), pipeline_mode=ONCE),
-            ANY,
-        ],
-        out_specs=[
-            pl.BlockSpec((tile, D), lambda i: (i, 0)),
-            pl.BlockSpec((2, PAD, RANK), lambda i: (0, 0, 0), pipeline_mode=ONCE),
-            ANY,
-        ],
-        out_shape=[
-            jax.ShapeDtypeStruct((rows, D), BF16),
-            jax.ShapeDtypeStruct((2, PAD, RANK), F32),
-            jax.ShapeDtypeStruct((DEV, PAD, RANK), F32),
-        ],
-        scratch_shapes=[
-            pltpu.VMEM((RANK, FFP), F32), pltpu.VMEM((FFP, RANK), F32), pltpu.VMEM((DEV, PAD, RANK), F32),
-            pltpu.VMEM((2,) + CUBE, F32), *stages(), *stages(),
-            dma((1,)), dma((3, 4)), dma((3, 4)), dma((3, 4)), dma((3, 4)),
-        ],
-        compiler_params=pltpu.CompilerParams(
-            dimension_semantics=("arbitrary",), collective_id=1, has_side_effects=True, vmem_limit_bytes=60000000),
-        cost_estimate=pl.CostEstimate(flops=31 * 10**9, bytes_accessed=70 * 10**6, transcendentals=0),
-        name="pass_c",
-    )(dh, dz, a0, w1, q, rx)
-
-
 def kernel_d(tile, tiles, width, chunks,
-             slope_ref, w2_ref, sum_ref, mu, vu, md, vd, g1_hbm, u0_hbm, rx_hbm,
+             slope_ref, w2_ref, mu, vu, md, vd, g1_hbm, u0_hbm, rx_hbm,
              mu_o, vu_o, md_o, vd_o, n_hbm,
              g1, u0, das, dz, acc_s, racc, rt, own_x, own_y,
-             x0, x1, x2, x3, y0, y1, y2, y3, gat, tmp, nb,
-             lsem, rx_s, rx_r, ry_s, ry_r, ag_s, ag_r, nsem):
+             xa0, xa1, xa2, xa3, xb0, xb1, xb2, xb3, xc0, xc1, xc2, xc3, y0, y1, y2, y3, gat, tmp, nb,
+             lsem, xa_s, xa_r, xb_s, xb_r, xc_s, xc_r, ry_s, ry_r, ag_s, ag_r, nsem):
     j = pl.program_id(0)
     slab = 16
     c = Comm()
     bits, core = c.bits, c.core
     ag_sems = (ag_s, ag_r)
-    flows_x = [(own_x, rx_hbm.at[1 - core], (x0, x1, x2, x3), (rx_s, rx_r), p) for p in range(3)]
+    bufs = ((xa0, xa1, xa2, xa3), (xb0, xb1, xb2, xb3), (xc0, xc1, xc2, xc3))
+    sems = ((xa_s, xa_r), (xb_s, xb_r), (xc_s, xc_r))
+    kinds = (1, 3, 2)
+    flows_x = [[(own_x.at[k], rx_hbm.at[k, 1 - core], bufs[k], sems[k], p) for p in THIRDS] for k in range(3)]
     flows_y = [(own_y.at[core], own_y.at[1 - core], (y0, y1, y2, y3), (ry_s, ry_r), p) for p in SIXTHS]
 
     def rs(flows, stage):
@@ -437,35 +360,48 @@
         n_copy(kind).start()
 
     def local(k):
-        src, dst = ((g1_hbm, g1), (u0_hbm, u0), (rx_hbm.at[core], own_x))[k]
+        src, dst = ((g1_hbm, g1), (u0_hbm, u0), (rx_hbm.at[:, core], own_x))[k]
         return pltpu.make_async_copy(src, dst, lsem.at[k])
 
     def begin():
         c.greet()
         for k in range(3):
             local(k).start()
-        adam(1, sum_ref[0, 0:SHARD, :])
-        adam(3, sum_ref[1, 0:SHARD, :])
         c.met()
-        ag((1, 3), 0)
-        for flow in flows_x:
-            c.rs_copy(flow, 0).start()
+        for k in range(3):
+            for flow in flows_x[k]:
+                c.rs_copy(flow, 0).start()
         for k in range(3):
             local(k).wait()
 
-    def step_one():
-        rs(flows_x, 0)
-        ag((1, 3), 1)
-
     def finish_x():
-        rs(flows_x, 3)
-        adam(2, own_x[bits[0], bits[1], bits[2], 0:SHARD, :])
-        ag((2,), 0)
-
-    events = {0: begin, 1: step_one, 2: lambda: ag((1, 3), 2), 3: lambda: rs(flows_x, 1), 4: lambda: ag((1, 3), 3),
-              5: lambda: rs(flows_x, 2), 7: finish_x, 8: lambda: ag((2,), 1), 9: lambda: ag((2,), 2), 10: lambda: ag((2,), 3)}
+        for k in range(3):
+            rs(flows_x[k], 3)
+            adam(kinds[k], own_x[k, bits[0], bits[1], bits[2], 0:SHARD, :])
+            ag((kinds[k],), 0)
+        add_y(0)
+
+    def all_zero():
+        for k in range(3):
+            rs(flows_x[k], 0)
+
+    def cross_y(z):
+        return c.remote(own_y.at[1 - core, z], y0.at[z], ry_s.at[z, 0], ry_r.at[z, 0], 3)
+
+    def early_y(z):
+        for d in range(8 * z, 8 * z + 8):
+            own_y[d % 2, z, d // 4 % 2, d // 2 % 2] = rt[SHARD * d:SHARD * d + PAD, :]
+        cross_y(z).start()
+
+    def add_y(z):
+        cross_y(z).wait()
+        own_y[core, z] = own_y[core, z] + y0[z]
+
+    events = {0: begin, 1: all_zero, 3: lambda: rs(flows_x[0], 1), 4: lambda: rs(flows_x[1], 1), 5: lambda: rs(flows_x[2], 1),
+              6: lambda: rs(flows_x[0], 2), 7: lambda: (rs(flows_x[1], 2), rs(flows_x[2], 2), early_y(0)),
+              8: finish_x, 9: lambda: ag(kinds, 1), 10: lambda: ag(kinds, 2)}
     for at, event in events.items():
-        pl.when(j == at)(event)
+        pl.when(j == at)(lambda event=event: [event(), None][1])
 
     now = lax.rem(j, 2)
 
@@ -497,19 +433,20 @@
     @pl.when(j == chunks - 1)
     def _():
         turn(j)
-        for d in range(DEV):
-            own_y[d % 2, d // 8, d // 4 % 2, d // 2 % 2] = rt[SHARD * d:SHARD * d + PAD, :]
+        early_y(1)
+        add_y(1)
         for flow in flows_y:
-            c.rs_copy(flow, 0).start()
-        ag((1, 3), 4)
+            c.rs_copy(flow, 1).start()
+        ag(kinds, 3)
+        rs(flows_y, 1)
+        ag((1,), 4)
         gather_rows(1)
-        rs(flows_y, 0)
+        rs(flows_y, 2)
         ag((2,), 4)
         gather_rows(2)
-        rs(flows_y, 1)
+        ag((3,), 4)
         n_copy(1).wait()
         gather_rows(3)
-        rs(flows_y, 2)
         rs(flows_y, 3)
         adam(0, own_y[core, bits[0], bits[1], bits[2], 0:SHARD, :])
         for stage in range(5):
@@ -520,8 +457,8 @@
         n_copy(0).wait()
 
 
-def call_d(z0, g1, u0, w2, sums, rx, mu, vu, md, vd):
-    rows, tile, width = z0.shape[0], 512, 256
+def call_d(slope, g1, u0, w2, rx, mu, vu, md, vd):
+    rows, tile, width = g1.shape[0], 512, 256
     chunks = FFP // width
     mom = jax.ShapeDtypeStruct((SHARD, 2, RANK), F32)
     momspec = pl.BlockSpec((SHARD, 2, RANK), lambda j: (0, 0, 0), pipeline_mode=ONCE)
@@ -530,9 +467,8 @@
         functools.partial(kernel_d, tile, rows // tile, width, chunks),
         grid=(chunks,),
         in_specs=[
-            pl.BlockSpec((rows, width), lambda j: (0, j)),
+            pl.BlockSpec((None, rows, width), lambda j: (j, 0, 0)),
             pl.BlockSpec((None, width, D), lambda j: (0, j, 0)),
-            pl.BlockSpec((2, PAD, RANK), lambda j: (0, 0, 0), pipeline_mode=ONCE),
             momspec, momspec, momspec, momspec, ANY, ANY, ANY,
         ],
         out_specs=[momspec] * 4 + [ANY],
@@ -541,15 +477,15 @@
             pltpu.VMEM((rows, D), BF16), pltpu.VMEM((RANK, rows), BF16),
             pltpu.VMEM((2, tile, width), F32), pltpu.VMEM((2, tile, width), BF16),
             pltpu.VMEM((RANK, width), F32), pltpu.VMEM((2, RANK, width), F32), pltpu.VMEM((FFP, RANK), F32),
-            pltpu.VMEM(CUBE, F32), pltpu.VMEM((2,) + CUBE, F32), *stages(), *stages(),
+            pltpu.VMEM((3,) + CUBE, F32), pltpu.VMEM((2,) + CUBE, F32), *stages(), *stages(), *stages(), *stages(),
             pltpu.VMEM((4, 2) + CUBE, BF16), pltpu.VMEM((FF, RANK), F32), pltpu.VMEM((2, FF, RANK), BF16),
-            dma((3,)), dma((3, 4)), dma((3, 4)), dma((9, 4)), dma((9, 4)), dma((4, 9, 7)), dma((4, 9, 7)), dma((4,)),
+            dma((3,)), *[dma((3, 4))] * 6, dma((9, 4)), dma((9, 4)), dma((4, 9, 7)), dma((4, 9, 7)), dma((4,)),
         ],
         compiler_params=pltpu.CompilerParams(
             dimension_semantics=("arbitrary",), collective_id=0, has_side_effects=True, vmem_limit_bytes=67000000),
         cost_estimate=pl.CostEstimate(flops=30 * 10**9, bytes_accessed=70 * 10**6, transcendentals=0),
         name="pass_d",
-    )(z0, w2, sums, mu, vu, md, vd, g1, u0, rx)
+    )(slope, w2, mu, vu, md, vd, g1, u0, rx)
 
 
 def kernel_w(count, part, wu_hbm, wd_hbm, n_hbm, p_ref, q_ref, nu_hbm, nd_hbm, buf, n, isem, nsem, osem):
@@ -620,11 +556,10 @@
 def solution(mesh):
     def local_step(x_loc, dh_loc, w_up, w_down, proj_up, proj_down, mom_up, var_up, mom_down, var_down):
         w_up_t = jnp.swapaxes(w_up, 1, 2)
-        z0, a0, dz1, u0, rx = call_a(x_loc, dh_loc, proj_up, proj_down, w_up_t, w_down)
-        g1, sums, ry = call_c(dh_loc, dz1, a0, w_up_t, proj_down, rx.reshape((2, 2) + CUBE))
+        slope, g1, u0, rx = call_a(x_loc, dh_loc, proj_up, proj_down, w_up_t, w_down)
         up, down = (2, 0, 1), (1, 0, 2)
         mu, vu, md, vd, dirs = call_d(
-            z0, g1, u0, w_down, sums, ry.reshape((2,) + CUBE), jnp.transpose(mom_up, up), jnp.transpose(var_up, up),
+            slope, g1, u0, w_down, rx.reshape((3, 2) + CUBE), jnp.transpose(mom_up, up), jnp.transpose(var_up, up),
             jnp.transpose(mom_down, down), jnp.transpose(var_down, down))
         new_mom_up, new_var_up = jnp.transpose(mu, (1, 2, 0)), jnp.transpose(vu, (1, 2, 0))
         new_mom_down, new_var_down = jnp.transpose(md, (1, 0, 2)), jnp.transpose(vd, (1, 0, 2))

time: 305 us -> 304 us (level)
    pallas_call x1 -> x0, Pallas kernels: 48.2 us -> none  [call_c(): pl.pallas_call(functools.partial(kernel_c, tile, tiles), grid=(tiles,), i...]
    pallas_call x1, Pallas kernels: 144 us -> 185 us  [call_a(): pl.pallas_call(functools.partial(kernel_a, tile, tiles), grid=(tiles,), i...]
    pallas_call x1, Pallas kernels: 90.4 us -> 95.7 us  [call_d(): pl.pallas_call(functools.partial(kernel_d, tile, rows // tile, width, chu...]
where the time goes in v3:
time: 304 us
  Pallas kernels  300 us (99%)
    pallas_call x1, Pallas kernels, call_a(): pl.pallas_call(functools.partial(kernel_a, tile, tiles), grid=(tiles,), i...  185 us
    pallas_call x1, Pallas kernels, call_d(): pl.pallas_call(functools.partial(kernel_d, tile, rows // tile, width, chu...  95.7 us
    pallas_call x1, Pallas kernels, call_w(): pl.pallas_call(functools.partial(kernel_w, count, part), in_specs=[ANY, A...  19 us

profile of v3, /device:TPU:0, one launch (start us, length us, event | category | flops | bytes accessed | tf_op | source)
XLA Modules:
  0.0 303.6 jit_solution(7466106083329960866)
XLA Ops:
  0.6 185.2 %pass_a.1 = (f32[11,4096,256]{2,1,0:T(8,128)}, bf16[4096,1024]{1,0:T(8,128)(2,1)}, bf16[256,4096]{1,0:T(8,128)(2,1)}, f32[3,16,176,256]{3,2,1,0:T(8,128)}) custom-call(bf16[4096,1024]{1,0:T(8,128)(2,1)} %x_ref.1, bf16[4096,1024]{1,0:T(8,128)(2,1)} %dh_ref.1, bf16[2,1024,256]{2,1,0:T(8,128)(2,1)} %p_ref.3, bf16[2,1024,256]{2,1,0:T(8,128)(2,1)} %q_ref.3, ...), custom_call_target="tpu_custom_call" | custom-call | flops 109999996928 | bytes 140000000 | tf_op jit(solution)/shard_map/pass_a/pallas_call | solution.py:190
  185.9 95.7 %pass_d.1 = (f32[171,2,256]{2,1,0:T(2,128)}, f32[171,2,256]{2,1,0:T(2,128)}, f32[171,2,256]{2,1,0:T(2,128)}, f32[171,2,256]{2,1,0:T(2,128)}, bf16[4,2736,256]{2,1,0:T(8,128)(2,1)}) custom-call(f32[11,4096,256]{2,1,0:T(8,128)} %get-tuple-element.17.slope_ref, bf16[2,2736,1024]{2,1,0:T(8,128)(2,1)} %w2_ref.1, f32[171,2,256]{2,1,0:T(2,128)} %bitcast.28, ...), custom_call_target="tpu_custom_call" | custom-call | flops 30000001024 | bytes 70000000 | tf_op jit(solution)/shard_map/pass_d/pallas_call | solution.py:466
  281.5 0.0 copy-start.3
  281.6 0.0 copy-start.2
  281.6 0.0 copy-start.1
  281.6 0.0 copy-start
  281.6 19.0 %pass_w.1 = (bf16[12,456,1024]{2,1,0:T(8,128)(2,1)}, bf16[12,456,1024]{2,1,0:T(8,128)(2,1)}) custom-call(bf16[12,456,1024]{2,1,0:T(8,128)(2,1)} %bitcast.19, bf16[12,456,1024]{2,1,0:T(8,128)(2,1)} %bitcast.20, bf16[24,456,256]{2,1,0:T(8,128)(2,1)} %bitcast.21, bf16[2,1024,256]{2,1,0:T(8,128)(2,1)} %p_ref.3, bf16[2,1024,256]{2,1,0:T(8,128)(2,1)} %q_ref.3), custom_call_target="tpu_custom_call" | custom-call | flops 6000000000 | bytes 50000000 | tf_op jit(solution)/shard_map/pass_w/pallas_call | solution.py:543
  300.6 0.0 copy-done.3
  300.6 0.7 copy.20
  301.4 0.0 copy-done.2
  301.4 0.7 copy.21
  302.1 0.0 copy-done.1
  302.1 0.7 copy.22
  302.8 0.0 copy-done
  302.8 0.7 copy.23
Async XLA Ops:
  281.5 19.1 %copy-start.3 = (f32[171,2,256]{2,1,0:T(2,128)S(1)}, f32[171,2,256]{2,1,0:T(2,128)}, u32[]{:S(2)}) copy-start(f32[171,2,256]{2,1,0:T(2,128)} %get-tuple-element.24) | copy-start | bytes 1050628
  281.6 19.8 %copy-start.2 = (f32[171,2,256]{2,1,0:T(2,128)S(1)}, f32[171,2,256]{2,1,0:T(2,128)}, u32[]{:S(2)}) copy-start(f32[171,2,256]{2,1,0:T(2,128)} %get-tuple-element.25) | copy-start | bytes 1050628
  281.6 20.5 %copy-start.1 = (f32[171,2,256]{2,1,0:T(2,128)S(1)}, f32[171,2,256]{2,1,0:T(2,128)}, u32[]{:S(2)}) copy-start(f32[171,2,256]{2,1,0:T(2,128)} %get-tuple-element.26) | copy-start | bytes 1050628
  281.6 21.2 %copy-start = (f32[171,2,256]{2,1,0:T(2,128)S(1)}, f32[171,2,256]{2,1,0:T(2,128)}, u32[]{:S(2)}) copy-start(f32[171,2,256]{2,1,0:T(2,128)} %get-tuple-element.27) | copy-start | bytes 1050628
